TPU v7x, 32 devices: a 4x4x1 block of a 4x4x8 slice. The times are simulated.
32 devices in a mesh: dp: 1 (over z), tp: 32 (over y, x, core).
Axes of the slice: x: 4, y: 4, z: 1, core: 2. Of those that a mesh axis runs over, the one named last changes fastest.
The devices are a block of a 4x4x8 slice.
Arguments:
- x_in: bfloat16 [2, 512, 2048], P(None, ('dp', 'tp'))
- y_cot: bfloat16 [2, 512, 2048], P(None, ('dp', 'tp'))
- gain_attn: float32 [2, 2048], replicated
- gain_mlp: float32 [2, 2048], replicated
- w_qkv: bfloat16 [2, 2048, 32, 3, 64], P(None, None, 'tp')
- w_out: bfloat16 [2, 32, 64, 2048], P(None, 'tp')
- w_gate: bfloat16 [2, 2048, 8192], P(None, None, 'tp')
- w_up: bfloat16 [2, 2048, 8192], P(None, None, 'tp')
- w_down: bfloat16 [2, 8192, 2048], P(None, 'tp')
Outputs:
- output 1: bfloat16 [2, 512, 2048], P(None, ('dp', 'tp'))
- output 2: bfloat16 [2, 512, 2048], P(None, ('dp', 'tp'))
- output 3: bfloat16 [2, 2048, 32, 3, 64], P('dp', None, 'tp')
- output 4: bfloat16 [2, 32, 64, 2048], P('dp', 'tp')
- output 5: bfloat16 [2, 2048, 8192], P('dp', None, 'tp')
- output 6: bfloat16 [2, 2048, 8192], P('dp', None, 'tp')
- output 7: bfloat16 [2, 8192, 2048], P('dp', 'tp')
- output 8: float32 [2, 2048], P('dp')
- output 9: float32 [2, 2048], P('dp')
All inputs are finite; a program needn't handle non-finite values.
Results may differ from a plain program's by a relative error of at most 0.02.
Values are sent between devices in bfloat16 or wider.
A program may use at most 768 MiB of HBM per device.

v0:
```python
import jax
import jax.numpy as jnp
from jax import lax
from jax.sharding import PartitionSpec as P

NORM_EPS = 1e-5


def rms_scale(row_vals, gain_vec):
    return row_vals * lax.rsqrt(jnp.mean(row_vals * row_vals, axis=-1, keepdims=True) + NORM_EPS) * gain_vec


def norm_apply(row_vals, gain_vec):
    return rms_scale(row_vals.astype(jnp.float32), gain_vec).astype(jnp.bfloat16)


def norm_backward(row_vals, gain_vec, cot_rows):
    unused, pull = jax.vjp(rms_scale, row_vals.astype(jnp.float32), gain_vec)
    return pull(cot_rows.astype(jnp.float32))


def causal_mask(seq_len):
    row_pos = lax.broadcasted_iota(jnp.int32, (seq_len, 1, seq_len), 0)
    col_pos = lax.broadcasted_iota(jnp.int32, (seq_len, 1, seq_len), 2)
    return row_pos >= col_pos


def attention_forward(queries, key_heads, value_heads, score_scale):
    seq_len = queries.shape[0]
    scores = jnp.einsum('qkge,tke->kqgt', queries, key_heads, preferred_element_type=jnp.float32) * score_scale
    scores = jnp.where(causal_mask(seq_len), scores, -1e30)
    row_max = jnp.max(scores, axis=-1, keepdims=True)
    exp_scores = jnp.exp(scores - row_max)
    row_total = jnp.sum(exp_scores, axis=-1, keepdims=True)
    prob_b16 = (exp_scores / row_total).astype(jnp.bfloat16)
    attn_mix = jnp.einsum('kqgt,tke->kqge', prob_b16, value_heads, preferred_element_type=jnp.float32).astype(jnp.bfloat16)
    return attn_mix, row_max + jnp.log(row_total)


def attention_backward(queries, key_heads, value_heads, log_norm, grad_mix, score_scale):
    seq_len = queries.shape[0]
    scores = jnp.einsum('qkge,tke->kqgt', queries, key_heads, preferred_element_type=jnp.float32) * score_scale
    scores = jnp.where(causal_mask(seq_len), scores, -1e30)
    prob_f32 = jnp.exp(scores - log_norm)
    prob_b16 = prob_f32.astype(jnp.bfloat16)
    grad_prob = jnp.einsum('qkge,tke->kqgt', grad_mix, value_heads, preferred_element_type=jnp.float32).astype(jnp.bfloat16).astype(jnp.float32)
    row_dot = jnp.sum(grad_prob * prob_f32, axis=-1, keepdims=True)
    grad_scores = (prob_f32 * (grad_prob - row_dot) * score_scale).astype(jnp.bfloat16)
    grad_q = jnp.einsum('kqgt,tke->qkge', grad_scores, key_heads, preferred_element_type=jnp.float32)
    grad_k = jnp.einsum('kqgt,qkge->tke', grad_scores, queries, preferred_element_type=jnp.float32)
    grad_v = jnp.einsum('kqgt,qkge->tke', prob_b16, grad_mix, preferred_element_type=jnp.float32)
    return grad_q, grad_k, grad_v


def solution(mesh):
    row_spec = P(None, ('dp', 'tp'), None)
    gain_spec = P(None, None)
    qkv_spec = P(None, None, 'tp', None, None)
    head_spec = P(None, 'tp', None, None)
    col_spec = P(None, None, 'tp')
    row_shard_spec = P(None, 'tp', None)

    def device_program(x_in, y_cot, gain_attn, gain_mlp, w_qkv, w_out, w_gate, w_up, w_down):
        micro_count = x_in.shape[0]
        width = x_in.shape[2]
        layer_count = w_qkv.shape[0]
        kv_local = w_qkv.shape[2]
        groups = w_qkv.shape[3] - 2
        head_dim = w_qkv.shape[4]
        score_scale = head_dim ** -0.5
        kept_acts = []
        y_rows = []
        for micro_idx in range(micro_count):
            layer_in = x_in[micro_idx]
            per_layer = []
            for layer_idx in range(layer_count):
                normed = norm_apply(layer_in, gain_attn[layer_idx])
                normed_full = lax.all_gather(normed, 'tp', axis=0, tiled=True)
                qkv_heads = jnp.einsum('sd,dkje->skje', normed_full, w_qkv[layer_idx], preferred_element_type=jnp.float32).astype(jnp.bfloat16)
                queries = qkv_heads[:, :, :groups]
                key_heads = qkv_heads[:, :, groups]
                value_heads = qkv_heads[:, :, groups + 1]
                attn_mix, log_norm = attention_forward(queries, key_heads, value_heads, score_scale)
                heads_out = w_out[layer_idx].reshape(kv_local, groups, head_dim, width)
                attn_part = jnp.einsum('kqge,kged->qd', attn_mix, heads_out, preferred_element_type=jnp.float32)
                attn_sum = lax.psum_scatter(attn_part, 'tp', scatter_dimension=0, tiled=True).astype(jnp.bfloat16)
                hidden = (layer_in.astype(jnp.float32) + attn_sum.astype(jnp.float32)).astype(jnp.bfloat16)
                normed_b = norm_apply(hidden, gain_mlp[layer_idx])
                normed_b_full = lax.all_gather(normed_b, 'tp', axis=0, tiled=True)
                gate_pre = jnp.dot(normed_b_full, w_gate[layer_idx], preferred_element_type=jnp.float32)
                up_proj = jnp.dot(normed_b_full, w_up[layer_idx], preferred_element_type=jnp.float32)
                inner = (jax.nn.silu(gate_pre) * up_proj).astype(jnp.bfloat16)
                down_part = jnp.dot(inner, w_down[layer_idx], preferred_element_type=jnp.float32)
                mlp_sum = lax.psum_scatter(down_part, 'tp', scatter_dimension=0, tiled=True).astype(jnp.bfloat16)
                per_layer.append((layer_in, normed, hidden, normed_b, queries, key_heads, value_heads, attn_mix, log_norm))
                layer_in = (hidden.astype(jnp.float32) + mlp_sum.astype(jnp.float32)).astype(jnp.bfloat16)
            kept_acts.append(per_layer)
            y_rows.append(layer_in)

        grad_qkv_acc = [None] * layer_count
        grad_out_acc = [None] * layer_count
        grad_gate_acc = [None] * layer_count
        grad_up_acc = [None] * layer_count
        grad_down_acc = [None] * layer_count
        gain_a_acc = [None] * layer_count
        gain_b_acc = [None] * layer_count

        def accumulate(acc_list, layer_idx, term):
            acc_list[layer_idx] = term if acc_list[layer_idx] is None else acc_list[layer_idx] + term

        grad_rows = []
        for micro_idx in range(micro_count):
            grad_in = y_cot[micro_idx]
            for layer_idx in reversed(range(layer_count)):
                layer_in, normed, hidden, normed_b, queries, key_heads, value_heads, attn_mix, log_norm = kept_acts[micro_idx][layer_idx]
                normed_b_full = lax.all_gather(normed_b, 'tp', axis=0, tiled=True)
                grad_full = lax.all_gather(grad_in, 'tp', axis=0, tiled=True)
                gate_pre = jnp.dot(normed_b_full, w_gate[layer_idx], preferred_element_type=jnp.float32)
                up_proj = jnp.dot(normed_b_full, w_up[layer_idx], preferred_element_type=jnp.float32)
                gate_sig = jax.nn.sigmoid(gate_pre)
                gate_act = gate_pre * gate_sig
                inner = (gate_act * up_proj).astype(jnp.bfloat16)
                accumulate(grad_down_acc, layer_idx, jnp.einsum('sf,sd->fd', inner, grad_full, preferred_element_type=jnp.float32))
                grad_inner = jnp.einsum('sd,fd->sf', grad_full, w_down[layer_idx], preferred_element_type=jnp.float32).astype(jnp.bfloat16).astype(jnp.float32)
                grad_up = (grad_inner * gate_act).astype(jnp.bfloat16)
                grad_gate = (grad_inner * up_proj * gate_sig * (1.0 + gate_pre * (1.0 - gate_sig))).astype(jnp.bfloat16)
                accumulate(grad_gate_acc, layer_idx, jnp.einsum('sd,sf->df', normed_b_full, grad_gate, preferred_element_type=jnp.float32))
                accumulate(grad_up_acc, layer_idx, jnp.einsum('sd,sf->df', normed_b_full, grad_up, preferred_element_type=jnp.float32))
                grad_nb_part = jnp.einsum('sf,df->sd', grad_gate, w_gate[layer_idx], preferred_element_type=jnp.float32) + jnp.einsum('sf,df->sd', grad_up, w_up[layer_idx], preferred_element_type=jnp.float32)
                grad_nb = lax.psum_scatter(grad_nb_part, 'tp', scatter_dimension=0, tiled=True).astype(jnp.bfloat16)
                grad_h_norm, grad_gain_b = norm_backward(hidden, gain_mlp[layer_idx], grad_nb)
                accumulate(gain_b_acc, layer_idx, grad_gain_b)
                grad_hidden = (grad_in.astype(jnp.float32) + grad_h_norm).astype(jnp.bfloat16)
                normed_full = lax.all_gather(normed, 'tp', axis=0, tiled=True)
                grad_hfull = lax.all_gather(grad_hidden, 'tp', axis=0, tiled=True)
                heads_out = w_out[layer_idx].reshape(kv_local, groups, head_dim, width)
                accumulate(grad_out_acc, layer_idx, jnp.einsum('kqge,qd->kged', attn_mix, grad_hfull, preferred_element_type=jnp.float32).reshape(w_out.shape[1:]))
                grad_mix = jnp.einsum('qd,kged->qkge', grad_hfull, heads_out, preferred_element_type=jnp.float32).astype(jnp.bfloat16)
                grad_q, grad_k, grad_v = attention_backward(queries, key_heads, value_heads, log_norm, grad_mix, score_scale)
                grad_qkv = jnp.concatenate([grad_q, grad_k[:, :, None], grad_v[:, :, None]], axis=2).astype(jnp.bfloat16)
                accumulate(grad_qkv_acc, layer_idx, jnp.einsum('sd,skje->dkje', normed_full, grad_qkv, preferred_element_type=jnp.float32))
                grad_n_part = jnp.einsum('skje,dkje->sd', grad_qkv, w_qkv[layer_idx], preferred_element_type=jnp.float32)
                grad_n = lax.psum_scatter(grad_n_part, 'tp', scatter_dimension=0, tiled=True).astype(jnp.bfloat16)
                grad_x_norm, grad_gain_a = norm_backward(layer_in, gain_attn[layer_idx], grad_n)
                accumulate(gain_a_acc, layer_idx, grad_gain_a)
                grad_in = (grad_hidden.astype(jnp.float32) + grad_x_norm).astype(jnp.bfloat16)
            grad_rows.append(grad_in)

        gain_grads = lax.psum(jnp.stack([jnp.stack(gain_a_acc), jnp.stack(gain_b_acc)]), 'tp')
        return (jnp.stack(y_rows), jnp.stack(grad_rows),
                jnp.stack([item.astype(jnp.bfloat16) for item in grad_qkv_acc]),
                jnp.stack([item.astype(jnp.bfloat16) for item in grad_out_acc]),
                jnp.stack([item.astype(jnp.bfloat16) for item in grad_gate_acc]),
                jnp.stack([item.astype(jnp.bfloat16) for item in grad_up_acc]),
                jnp.stack([item.astype(jnp.bfloat16) for item in grad_down_acc]),
                gain_grads[0], gain_grads[1])

    return jax.shard_map(device_program, mesh=mesh,
                         in_specs=(row_spec, row_spec, gain_spec, gain_spec, qkv_spec, head_spec, col_spec, col_spec, row_shard_spec),
                         out_specs=(row_spec, row_spec, P('dp', None, 'tp', None, None), P('dp', 'tp', None, None), P('dp', None, 'tp'), P('dp', None, 'tp'), P('dp', 'tp', None), P('dp', None), P('dp', None)),
                         check_vma=False)
```

profile of v0, /device:TPU:97, one launch (start us, length us, event | category | flops | bytes accessed | tf_op | source)
XLA Modules:
  0.0 1962.6 jit_solution(15033541131257895137)
XLA Ops:
  15.2 39.4 %all-gather.19.cloned.1.call-done = bf16[512,2048]{1,0:T(8,128)(2,1)} async-done(((bf16[16,2048]{1,0:T(8,128)(2,1)}), bf16[512,2048]{1,0:T(8,128)(2,1)}) %all-gather.19.cloned.1.call-update) | async-done | bytes 2097168 | tf_op jit(solution)/shard_map/all_gather | solution.py:78
  61.6 33.3 %all-gather.27.cloned.1.call-done = bf16[512,2048]{1,0:T(8,128)(2,1)} async-done(((bf16[16,2048]{1,0:T(8,128)(2,1)}), bf16[512,2048]{1,0:T(8,128)(2,1)}) %all-gather.27.cloned.1.call-update) | async-done | bytes 2097168 | tf_op jit(solution)/shard_map/all_gather | solution.py:78
  102.2 67.9 %reduce-scatter.17.cloned.1.call-done = f32[16,2048]{1,0:T(8,128)} async-done(((f32[512,2048]{1,0:T(8,128)}), f32[16,2048]{1,0:T(8,128)}) %reduce-scatter.17.cloned.1.call-update) | async-done | bytes 131088 | tf_op jit(solution)/shard_map/reduce_scatter | solution.py:86
  170.0 77.2 %reduce-scatter.25.cloned.1.call-done = f32[16,2048]{1,0:T(8,128)} async-done(((f32[512,2048]{1,0:T(8,128)}), f32[16,2048]{1,0:T(8,128)}) %reduce-scatter.25.cloned.1.call-update) | async-done | bytes 131088 | tf_op jit(solution)/shard_map/reduce_scatter | solution.py:86
  250.5 39.1 %all-gather.29.cloned.1.call-done = bf16[512,2048]{1,0:T(8,128)(2,1)} async-done(((bf16[16,2048]{1,0:T(8,128)(2,1)}), bf16[512,2048]{1,0:T(8,128)(2,1)}) %all-gather.29.cloned.1.call-update) | async-done | bytes 2097168 | tf_op jit(solution)/shard_map/all_gather | solution.py:89
  297.5 32.2 %all-gather.21.cloned.1.call-done = bf16[512,2048]{1,0:T(8,128)(2,1)} async-done(((bf16[16,2048]{1,0:T(8,128)(2,1)}), bf16[512,2048]{1,0:T(8,128)(2,1)}) %all-gather.21.cloned.1.call-update) | async-done | bytes 2097168 | tf_op jit(solution)/shard_map/all_gather | solution.py:89
  339.0 65.9 %reduce-scatter.27.cloned.1.call-done = f32[16,2048]{1,0:T(8,128)} async-done(((f32[512,2048]{1,0:T(8,128)}), f32[16,2048]{1,0:T(8,128)}) %reduce-scatter.27.cloned.1.call-update) | async-done | bytes 131088 | tf_op jit(solution)/shard_map/reduce_scatter | solution.py:94
  406.5 75.8 %reduce-scatter.19.cloned.1.call-done = f32[16,2048]{1,0:T(8,128)} async-done(((f32[512,2048]{1,0:T(8,128)}), f32[16,2048]{1,0:T(8,128)}) %reduce-scatter.19.cloned.1.call-update) | async-done | bytes 131088 | tf_op jit(solution)/shard_map/reduce_scatter | solution.py:94
  485.4 39.8 %all-gather.23.cloned.1.call-done = bf16[512,2048]{1,0:T(8,128)(2,1)} async-done(((bf16[16,2048]{1,0:T(8,128)(2,1)}), bf16[512,2048]{1,0:T(8,128)(2,1)}) %all-gather.23.cloned.1.call-update) | async-done | bytes 2097168 | tf_op jit(solution)/shard_map/all_gather | solution.py:78
  534.9 70.5 %reduce-scatter.21.cloned.1.call-done = f32[16,2048]{1,0:T(8,128)} async-done(((f32[512,2048]{1,0:T(8,128)}), f32[16,2048]{1,0:T(8,128)}) %reduce-scatter.21.cloned.1.call-update) | async-done | bytes 131088 | tf_op jit(solution)/shard_map/reduce_scatter | solution.py:86
  610.1 37.8 %all-gather.31.cloned.1.call-done = bf16[512,2048]{1,0:T(8,128)(2,1)} async-done(((bf16[16,2048]{1,0:T(8,128)(2,1)}), bf16[512,2048]{1,0:T(8,128)(2,1)}) %all-gather.31.cloned.1.call-update) | async-done | bytes 2097168 | tf_op jit(solution)/shard_map/all_gather | solution.py:78
  656.3 31.0 %all-gather.25.cloned.1.call-done = bf16[512,2048]{1,0:T(8,128)(2,1)} async-done(((bf16[16,2048]{1,0:T(8,128)(2,1)}), bf16[512,2048]{1,0:T(8,128)(2,1)}) %all-gather.25.cloned.1.call-update) | async-done | bytes 2097168 | tf_op jit(solution)/shard_map/all_gather | solution.py:89
  692.3 34.6 %all-gather.47.cloned.1.call-done = bf16[1,512,2048]{2,1,0:T(8,128)(2,1)} async-done(((bf16[1,16,2048]{2,1,0:T(8,128)(2,1)}), bf16[1,512,2048]{2,1,0:T(8,128)(2,1)}) %all-gather.47.cloned.1.call-update) | async-done | bytes 2097168 | tf_op jit(solution)/shard_map/all_gather | solution.py:117
  735.5 66.4 %reduce-scatter.29.cloned.1.call-done = f32[16,2048]{1,0:T(8,128)} async-done(((f32[512,2048]{1,0:T(8,128)}), f32[16,2048]{1,0:T(8,128)}) %reduce-scatter.29.cloned.1.call-update) | async-done | bytes 131088 | tf_op jit(solution)/shard_map/reduce_scatter | solution.py:86
  804.6 74.6 %reduce-scatter.33.cloned.1.call-done = f32[16,2048]{1,0:T(8,128)} async-done(((f32[512,2048]{1,0:T(8,128)}), f32[16,2048]{1,0:T(8,128)}) %reduce-scatter.33.cloned.1.call-update) | async-done | bytes 131088 | tf_op jit(solution)/shard_map/reduce_scatter | solution.py:130
  882.3 39.1 %all-gather.33.cloned.1.call-done = bf16[512,2048]{1,0:T(8,128)(2,1)} async-done(((bf16[16,2048]{1,0:T(8,128)(2,1)}), bf16[512,2048]{1,0:T(8,128)(2,1)}) %all-gather.33.cloned.1.call-update) | async-done | bytes 2097168 | tf_op jit(solution)/shard_map/all_gather | solution.py:89
  926.5 34.4 %all-gather.49.cloned.1.call-done = bf16[1,512,2048]{2,1,0:T(8,128)(2,1)} async-done(((bf16[1,16,2048]{2,1,0:T(8,128)(2,1)}), bf16[1,512,2048]{2,1,0:T(8,128)(2,1)}) %all-gather.49.cloned.1.call-update) | async-done | bytes 2097168 | tf_op jit(solution)/shard_map/all_gather | solution.py:117
  979.0 62.1 %reduce-scatter.41.cloned.1.call-done = f32[16,2048]{1,0:T(8,128)} async-done(((f32[512,2048]{1,0:T(8,128)}), f32[16,2048]{1,0:T(8,128)}) %reduce-scatter.41.cloned.1.call-update) | async-done | bytes 131088 | tf_op jit(solution)/shard_map/reduce_scatter | solution.py:130
  1044.0 74.6 %reduce-scatter.23.cloned.1.call-done = f32[16,2048]{1,0:T(8,128)} async-done(((f32[512,2048]{1,0:T(8,128)}), f32[16,2048]{1,0:T(8,128)}) %reduce-scatter.23.cloned.1.call-update) | async-done | bytes 131088 | tf_op jit(solution)/shard_map/reduce_scatter | solution.py:94
  1118.6 77.2 %reduce-scatter.31.cloned.1.call-done = f32[16,2048]{1,0:T(8,128)} async-done(((f32[512,2048]{1,0:T(8,128)}), f32[16,2048]{1,0:T(8,128)}) %reduce-scatter.31.cloned.1.call-update) | async-done | bytes 131088 | tf_op jit(solution)/shard_map/reduce_scatter | solution.py:94
  1199.6 38.6 %all-gather.41.cloned.1.call-done = bf16[512,2048]{1,0:T(8,128)(2,1)} async-done(((bf16[16,2048]{1,0:T(8,128)(2,1)}), bf16[512,2048]{1,0:T(8,128)(2,1)}) %all-gather.41.cloned.1.call-update) | async-done | bytes 2097168 | tf_op jit(solution)/shard_map/all_gather | solution.py:135
  1247.1 31.3 %all-gather.35.cloned.1.call-done = bf16[512,2048]{1,0:T(8,128)(2,1)} async-done(((bf16[16,2048]{1,0:T(8,128)(2,1)}), bf16[512,2048]{1,0:T(8,128)(2,1)}) %all-gather.35.cloned.1.call-update) | async-done | bytes 2097168 | tf_op jit(solution)/shard_map/all_gather | solution.py:135
  1286.1 67.4 %reduce-scatter.43.cloned.1.call-done = f32[16,2048]{1,0:T(8,128)} async-done(((f32[512,2048]{1,0:T(8,128)}), f32[16,2048]{1,0:T(8,128)}) %reduce-scatter.43.cloned.1.call-update) | async-done | bytes 131088 | tf_op jit(solution)/shard_map/reduce_scatter | solution.py:143
  1353.6 77.2 %reduce-scatter.35.cloned.1.call-done = f32[16,2048]{1,0:T(8,128)} async-done(((f32[512,2048]{1,0:T(8,128)}), f32[16,2048]{1,0:T(8,128)}) %reduce-scatter.35.cloned.1.call-update) | async-done | bytes 131088 | tf_op jit(solution)/shard_map/reduce_scatter | solution.py:143
  1436.4 39.2 %all-gather.43.cloned.1.call-done = bf16[512,2048]{1,0:T(8,128)(2,1)} async-done(((bf16[16,2048]{1,0:T(8,128)(2,1)}), bf16[512,2048]{1,0:T(8,128)(2,1)}) %all-gather.43.cloned.1.call-update) | async-done | bytes 2097168 | tf_op jit(solution)/shard_map/all_gather | solution.py:117
  1483.4 32.2 %all-gather.37.cloned.1.call-done = bf16[512,2048]{1,0:T(8,128)(2,1)} async-done(((bf16[16,2048]{1,0:T(8,128)(2,1)}), bf16[512,2048]{1,0:T(8,128)(2,1)}) %all-gather.37.cloned.1.call-update) | async-done | bytes 2097168 | tf_op jit(solution)/shard_map/all_gather | solution.py:117
  1523.4 67.2 %reduce-scatter.45.cloned.1.call-done = f32[16,2048]{1,0:T(8,128)} async-done(((f32[512,2048]{1,0:T(8,128)}), f32[16,2048]{1,0:T(8,128)}) %reduce-scatter.45.cloned.1.call-update) | async-done | bytes 131088 | tf_op jit(solution)/shard_map/reduce_scatter | solution.py:130
  1590.6 77.4 %reduce-scatter.37.cloned.1.call-done = f32[16,2048]{1,0:T(8,128)} async-done(((f32[512,2048]{1,0:T(8,128)}), f32[16,2048]{1,0:T(8,128)}) %reduce-scatter.37.cloned.1.call-update) | async-done | bytes 131088 | tf_op jit(solution)/shard_map/reduce_scatter | solution.py:130
  1674.3 38.5 %all-gather.45.cloned.1.call-done = bf16[512,2048]{1,0:T(8,128)(2,1)} async-done(((bf16[16,2048]{1,0:T(8,128)(2,1)}), bf16[512,2048]{1,0:T(8,128)(2,1)}) %all-gather.45.cloned.1.call-update) | async-done | bytes 2097168 | tf_op jit(solution)/shard_map/all_gather | solution.py:135
  1784.7 43.3 %reduce-scatter.47.cloned.1.call-done = f32[16,2048]{1,0:T(8,128)} async-done(((f32[512,2048]{1,0:T(8,128)}), f32[16,2048]{1,0:T(8,128)}) %reduce-scatter.47.cloned.1.call-update) | async-done | bytes 131088 | tf_op jit(solution)/shard_map/reduce_scatter | solution.py:143
  1828.0 77.4 %reduce-scatter.39.cloned.1.call-done = f32[16,2048]{1,0:T(8,128)} async-done(((f32[512,2048]{1,0:T(8,128)}), f32[16,2048]{1,0:T(8,128)}) %reduce-scatter.39.cloned.1.call-update) | async-done | bytes 131088 | tf_op jit(solution)/shard_map/reduce_scatter | solution.py:143
  1906.7 46.4 %psum.7 = f32[2,2,2048]{2,1,0:T(2,128)S(1)} all-reduce(f32[2,2,2048]{2,1,0:T(2,128)S(1)} %pad_maximum_fusion.11), channel_id=1, replica_groups=mesh['dp'=1,'tp'=32] {'tp'}, use_global_device_ids=true, to_apply=%region_52.53 | all-reduce | flops 8192 | bytes 65536 | tf_op jit(solution)/shard_map/psum | solution.py:149
  (542 shorter events, 237.5 us)
Async XLA Ops:
  7.2 47.5 %all-gather.19.cloned.1.call-start = ((), (), s32[]{:S(2)}) async-start(), calls=%async_computation.16 | async-start | bytes 2162688 | tf_op jit(solution)/shard_map/all_gather | solution.py:78
  11.9 82.9 %all-gather.27.cloned.1.call-start = ((), (), s32[]{:S(2)}) async-start(), calls=%async_computation.24 | async-start | bytes 2162688 | tf_op jit(solution)/shard_map/all_gather | solution.py:78
  12.7 157.3 %reduce-scatter.17.cloned.1.call-start = ((), (), s32[]{:S(2)}) async-start(), calls=%async_computation.17 | async-start | bytes 4325376 | tf_op jit(solution)/shard_map/reduce_scatter | solution.py:86
  61.5 185.8 %reduce-scatter.25.cloned.1.call-start = ((), (), s32[]{:S(2)}) async-start(), calls=%async_computation.25 | async-start | bytes 4325376 | tf_op jit(solution)/shard_map/reduce_scatter | solution.py:86
  101.5 188.2 %all-gather.29.cloned.1.call-start = ((), (), s32[]{:S(2)}) async-start(), calls=%async_computation.26 | async-start | bytes 2162688 | tf_op jit(solution)/shard_map/all_gather | solution.py:89
  249.8 79.9 %all-gather.21.cloned.1.call-start = ((), (), s32[]{:S(2)}) async-start(), calls=%async_computation.18 | async-start | bytes 2162688 | tf_op jit(solution)/shard_map/all_gather | solution.py:89
  250.5 154.4 %reduce-scatter.27.cloned.1.call-start = ((), (), s32[]{:S(2)}) async-start(), calls=%async_computation.27 | async-start | bytes 4325376 | tf_op jit(solution)/shard_map/reduce_scatter | solution.py:94
  297.5 184.8 %reduce-scatter.19.cloned.1.call-start = ((), (), s32[]{:S(2)}) async-start(), calls=%async_computation.19 | async-start | bytes 4325376 | tf_op jit(solution)/shard_map/reduce_scatter | solution.py:94
  339.0 186.2 %all-gather.23.cloned.1.call-start = ((), (), s32[]{:S(2)}) async-start(), calls=%async_computation.20 | async-start | bytes 2162688 | tf_op jit(solution)/shard_map/all_gather | solution.py:78
  485.3 120.1 %reduce-scatter.21.cloned.1.call-start = ((), (), s32[]{:S(2)}) async-start(), calls=%async_computation.21 | async-start | bytes 4325376 | tf_op jit(solution)/shard_map/reduce_scatter | solution.py:86
  533.6 114.2 %all-gather.31.cloned.1.call-start = ((), (), s32[]{:S(2)}) async-start(), calls=%async_computation.28 | async-start | bytes 2162688 | tf_op jit(solution)/shard_map/all_gather | solution.py:78
  534.4 152.9 %all-gather.25.cloned.1.call-start = ((), (), s32[]{:S(2)}) async-start(), calls=%async_computation.22 | async-start | bytes 2162688 | tf_op jit(solution)/shard_map/all_gather | solution.py:89
  608.3 118.6 %all-gather.47.cloned.1.call-start = ((), (), s32[]{:S(2)}) async-start(), calls=%async_computation.46 | async-start | bytes 2162688 | tf_op jit(solution)/shard_map/all_gather | solution.py:117
  610.0 192.0 %reduce-scatter.29.cloned.1.call-start = ((), (), s32[]{:S(2)}) async-start(), calls=%async_computation.29 | async-start | bytes 4325376 | tf_op jit(solution)/shard_map/reduce_scatter | solution.py:86
  656.2 223.0 %reduce-scatter.33.cloned.1.call-start = ((), (), s32[]{:S(2)}) async-start(), calls=%async_computation.32 | async-start | bytes 4325376 | tf_op jit(solution)/shard_map/reduce_scatter | solution.py:130
  735.4 186.0 %all-gather.33.cloned.1.call-start = ((), (), s32[]{:S(2)}) async-start(), calls=%async_computation.30 | async-start | bytes 2162688 | tf_op jit(solution)/shard_map/all_gather | solution.py:89
  881.6 79.3 %all-gather.49.cloned.1.call-start = ((), (), s32[]{:S(2)}) async-start(), calls=%async_computation.47 | async-start | bytes 2162688 | tf_op jit(solution)/shard_map/all_gather | solution.py:117
  882.2 159.0 %reduce-scatter.41.cloned.1.call-start = ((), (), s32[]{:S(2)}) async-start(), calls=%async_computation.39 | async-start | bytes 4325376 | tf_op jit(solution)/shard_map/reduce_scatter | solution.py:130
  969.3 149.2 %reduce-scatter.23.cloned.1.call-start = ((), (), s32[]{:S(2)}) async-start(), calls=%async_computation.23 | async-start | bytes 4325376 | tf_op jit(solution)/shard_map/reduce_scatter | solution.py:94
  973.5 222.3 %reduce-scatter.31.cloned.1.call-start = ((), (), s32[]{:S(2)}) async-start(), calls=%async_computation.31 | async-start | bytes 4325376 | tf_op jit(solution)/shard_map/reduce_scatter | solution.py:94
  977.7 260.5 %all-gather.41.cloned.1.call-start = ((), (), s32[]{:S(2)}) async-start(), calls=%async_computation.40 | async-start | bytes 2162688 | tf_op jit(solution)/shard_map/all_gather | solution.py:135
  1197.8 80.5 %all-gather.35.cloned.1.call-start = ((), (), s32[]{:S(2)}) async-start(), calls=%async_computation.33 | async-start | bytes 2162688 | tf_op jit(solution)/shard_map/all_gather | solution.py:135
  1198.7 154.9 %reduce-scatter.43.cloned.1.call-start = ((), (), s32[]{:S(2)}) async-start(), calls=%async_computation.41 | async-start | bytes 4325376 | tf_op jit(solution)/shard_map/reduce_scatter | solution.py:143
  1245.8 185.0 %reduce-scatter.35.cloned.1.call-start = ((), (), s32[]{:S(2)}) async-start(), calls=%async_computation.34 | async-start | bytes 4325376 | tf_op jit(solution)/shard_map/reduce_scatter | solution.py:143
  1286.1 189.5 %all-gather.43.cloned.1.call-start = ((), (), s32[]{:S(2)}) async-start(), calls=%async_computation.42 | async-start | bytes 2162688 | tf_op jit(solution)/shard_map/all_gather | solution.py:117
  1435.7 79.9 %all-gather.37.cloned.1.call-start = ((), (), s32[]{:S(2)}) async-start(), calls=%async_computation.35 | async-start | bytes 2162688 | tf_op jit(solution)/shard_map/all_gather | solution.py:117
  1436.3 154.3 %reduce-scatter.45.cloned.1.call-start = ((), (), s32[]{:S(2)}) async-start(), calls=%async_computation.43 | async-start | bytes 4325376 | tf_op jit(solution)/shard_map/reduce_scatter | solution.py:130
  1483.3 184.7 %reduce-scatter.37.cloned.1.call-start = ((), (), s32[]{:S(2)}) async-start(), calls=%async_computation.36 | async-start | bytes 4325376 | tf_op jit(solution)/shard_map/reduce_scatter | solution.py:130
  1523.3 189.4 %all-gather.45.cloned.1.call-start = ((), (), s32[]{:S(2)}) async-start(), calls=%async_computation.44 | async-start | bytes 2162688 | tf_op jit(solution)/shard_map/all_gather | solution.py:135
  1672.9 80.0 %all-gather.39.cloned.1.call-start = ((), (), s32[]{:S(2)}) async-start(), calls=%async_computation.37 | async-start | bytes 2162688 | tf_op jit(solution)/shard_map/all_gather | solution.py:135
  1673.5 154.5 %reduce-scatter.47.cloned.1.call-start = ((), (), s32[]{:S(2)}) async-start(), calls=%async_computation.45 | async-start | bytes 4325376 | tf_op jit(solution)/shard_map/reduce_scatter | solution.py:143
  1720.4 185.0 %reduce-scatter.39.cloned.1.call-start = ((), (), s32[]{:S(2)}) async-start(), calls=%async_computation.38 | async-start | bytes 4325376 | tf_op jit(solution)/shard_map/reduce_scatter | solution.py:143
  (160 other events, 2802.3 us)
Sparse Core Ops, SparseCore 0:
  12.1 42.5 all-gather.18
  57.3 37.4 all-gather.26
  98.3 71.6 reduce-scatter.16
  173.4 73.8 reduce-scatter.24
  249.9 39.6 all-gather.28
  292.2 37.4 all-gather.20
  333.2 71.6 reduce-scatter.26
  408.4 73.8 reduce-scatter.18
  485.4 39.7 all-gather.22
  533.7 71.6 reduce-scatter.20
  608.1 39.7 all-gather.30
  649.8 37.4 all-gather.24
  689.4 37.4 all-gather.46
  730.2 71.6 reduce-scatter.28
  805.3 73.8 reduce-scatter.32
  881.7 39.7 all-gather.32
  923.4 37.4 all-gather.48
  969.5 71.6 reduce-scatter.40
  1044.6 73.8 reduce-scatter.22
  1121.9 73.8 reduce-scatter.30
  1198.5 39.7 all-gather.40
  1240.9 37.4 all-gather.34
  1281.9 71.6 reduce-scatter.42
  1356.9 73.8 reduce-scatter.34
  1435.8 39.6 all-gather.42
  1478.1 37.4 all-gather.36
  1518.9 71.6 reduce-scatter.44
  1594.1 73.8 reduce-scatter.36
  1673.0 39.7 all-gather.44
  1715.2 37.5 all-gather.38
  1756.3 71.6 reduce-scatter.46
  1831.5 73.8 reduce-scatter.38
where the time goes:
time: 1970 us; the launch traced here: 1960 us
  waiting for transfers between devices  1690 us (86%)
  matrix products  130 us (7%)
  other arithmetic  47.7 us (2%)
  blocking collectives  46.4 us (2%)
  local copies, waits for them, and re-layouts  33.1 us (2%)
    reduce_scatter x4, waiting for transfers between devices, device_program(): lax.psum_scatter(down_part, 'tp', scatter_dimension=0, tiled=True)  293 us
    reduce_scatter x4, waiting for transfers between devices, device_program(): lax.psum_scatter(attn_part, 'tp', scatter_dimension=0, tiled=True)  282 us
    reduce_scatter x4, waiting for transfers between devices, device_program(): lax.psum_scatter(grad_nb_part, 'tp', scatter_dimension=0, tiled=True)  281 us
    reduce_scatter x4, waiting for transfers between devices, device_program(): lax.psum_scatter(grad_n_part, 'tp', scatter_dimension=0, tiled=True)  265 us
    all_gather x4, waiting for transfers between devices, device_program(): normed_full = lax.all_gather(normed, 'tp', axis=0, tiled=True)  150 us
    all_gather x4, waiting for transfers between devices, device_program(): normed_b_full = lax.all_gather(normed_b, 'tp', axis=0, tiled=True)  141 us
    all_gather x4, waiting for transfers between devices, device_program(): grad_full = lax.all_gather(grad_in, 'tp', axis=0, tiled=True)  140 us
    all_gather x4, waiting for transfers between devices, device_program(): grad_hfull = lax.all_gather(grad_hidden, 'tp', axis=0, tiled=True)  126 us
  transfers between devices with their start and end apart: 32, of which 32 were waited for; matrix products, arithmetic and copies ran while one was open for 7% of the time, Pallas kernels for 0%

commit v1 on v0

v1 whole, which is shorter than its diff:
```python
import functools
import math

import jax
import jax.numpy as jnp
from jax import lax
from jax.experimental import pallas as pl
from jax.experimental.pallas import tpu as pltpu
from jax.sharding import PartitionSpec as P

NORM_EPS = 1e-5
MESH = pl.DeviceIdType.MESH
CORES = 2
F32 = jnp.float32
B16 = jnp.bfloat16


def rms_scale(row_vals, gain_vec):
    return row_vals * lax.rsqrt(jnp.mean(row_vals * row_vals, axis=-1, keepdims=True) + NORM_EPS) * gain_vec


class Place:
    def __init__(self, side):
        me = lax.axis_index('tp')
        self.side = side
        self.core = lax.rem(me, CORES)
        chip = lax.div(me, CORES)
        self.x = lax.rem(chip, side)
        self.y = lax.div(chip, side)
        self.partner = self.dev(self.y, self.x, 1 - self.core)

    def dev(self, y, x, core):
        return {'tp': (y * self.side + x) * CORES + core}

    def shift(self, coord, by):
        return lax.rem(coord + by + self.side, self.side)

    def on_ring(self, axis, by):
        if axis == 0:
            return self.dev(self.y, self.shift(self.x, by), self.core)
        return self.dev(self.shift(self.y, by), self.x, self.core)


class Copies:
    def __init__(self, send_sems, recv_sems):
        self.send_sems = send_sems
        self.recv_sems = recv_sems
        self.started = []

    def start(self, src, dst, target):
        idx = len(self.started)
        copy = pltpu.make_async_remote_copy(src_ref=src, dst_ref=dst, send_sem=self.send_sems.at[idx],
                                            recv_sem=self.recv_sems.at[idx], device_id=target, device_id_type=MESH)
        copy.start()
        self.started.append(copy)
        return copy

    def finish(self):
        for copy in self.started:
            copy.wait_send()


def entry_barrier(place, far):
    targets = [place.partner]
    for axis in (0, 1):
        for by in (1, -1) + ((2,) if far else ()):
            targets.append(place.on_ring(axis, by))
    barrier = pltpu.get_barrier_semaphore()
    for target in targets:
        pl.semaphore_signal(barrier, inc=1, device_id=target, device_id_type=MESH)
    pl.semaphore_wait(barrier, len(targets))


def add_rows(dst, *terms):
    def body(i, carry):
        total = terms[0][i]
        for term in terms[1:]:
            total = total + term[i]
        dst[i] = total
        return carry
    lax.fori_loop(0, dst.shape[0], body, 0)


def reduce_scatter(place, copies, pairs, send_buf, own_buf, chip_buf, ring_buf, tail_buf, sums, mm_cols):
    side = place.side
    micro = sums.shape[0]
    rows = sums.shape[1]
    half_cols = sums.shape[2] // 2

    def products(half, core, buf):
        for m in range(micro):
            for start in range(0, half_cols, mm_cols):
                cols = pl.ds(half * half_cols + start, mm_cols)
                total = None
                for a_ref, b_ref, transposed in pairs:
                    left = a_ref[m, core]
                    if transposed:
                        part = lax.dot_general(left, b_ref[cols, :], (((1,), (1,)), ((), ())), preferred_element_type=F32)
                    else:
                        part = jnp.dot(left, b_ref[:, cols], preferred_element_type=F32)
                    total = part if total is None else total + part
                total = total.reshape(side, side, rows, mm_cols)
                for yy in range(side):
                    for xx in range(side):
                        first, second = (xx, yy) if half == 0 else (yy, xx)
                        buf[half, first, m, second, :, start:start + mm_cols] = total[yy, xx]

    spots = []
    chip_copies = {}
    for half in (0, 1):
        coord = place.x if half == 0 else place.y
        spots.append((coord, place.shift(coord, 1), place.shift(coord, -1), place.shift(coord, 2)))
    for half in (0, 1):
        products(half, 1 - place.core, send_buf)
        here, plus, minus, far = spots[half]
        for name, spot in (('far', far), ('plus', plus), ('minus', minus), ('here', here)):
            chip_copies[half, name] = copies.start(send_buf.at[half, spot], chip_buf.at[half, spot], place.partner)
    for half in (0, 1):
        products(half, place.core, own_buf)

    def join(half, name, spot):
        chip_copies[half, name].wait_recv()
        for m in range(micro):
            add_rows(own_buf.at[half, spot, m], own_buf.at[half, spot, m], chip_buf.at[half, spot, m])

    first = {}
    for half in (0, 1):
        here, plus, minus, far = spots[half]
        join(half, 'far', far)
        first[half, 0] = copies.start(own_buf.at[half, far, 0], ring_buf.at[half, 0], place.on_ring(half, 1))
        first[half, 1] = copies.start(own_buf.at[half, far, 1], ring_buf.at[half, 1], place.on_ring(half, -1))
    for half in (0, 1):
        here, plus, minus, far = spots[half]
        join(half, 'plus', plus)
        first[half, 2] = copies.start(own_buf.at[half, plus, 1], ring_buf.at[half, 2], place.on_ring(half, 1))
        join(half, 'minus', minus)
        first[half, 3] = copies.start(own_buf.at[half, minus, 0], ring_buf.at[half, 3], place.on_ring(half, -1))
    for half in (0, 1):
        join(half, 'here', spots[half][0])
    for half in (0, 1):
        here, plus, minus, far = spots[half]
        first[half, 0].wait_recv()
        add_rows(own_buf.at[half, plus, 0], own_buf.at[half, plus, 0], ring_buf.at[half, 0])
        first[half, 4] = copies.start(own_buf.at[half, plus, 0], ring_buf.at[half, 4], place.on_ring(half, 1))
        first[half, 1].wait_recv()
        add_rows(own_buf.at[half, minus, 1], own_buf.at[half, minus, 1], ring_buf.at[half, 1])
        first[half, 5] = copies.start(own_buf.at[half, minus, 1], ring_buf.at[half, 5], place.on_ring(half, -1))
    second = {}
    for half in (0, 1):
        here = spots[half][0]
        axis = 1 - half
        _, plus, minus, far = spots[axis]
        for slot in (2, 3, 4, 5):
            first[half, slot].wait_recv()
        add_rows(own_buf.at[half, here, 0], own_buf.at[half, here, 0], ring_buf.at[half, 3], ring_buf.at[half, 4])
        add_rows(own_buf.at[half, here, 1], own_buf.at[half, here, 1], ring_buf.at[half, 2], ring_buf.at[half, 5])
        second[half, 0] = copies.start(own_buf.at[half, here, 0, far], tail_buf.at[half, 0], place.on_ring(axis, 1))
        second[half, 1] = copies.start(own_buf.at[half, here, 1, far], tail_buf.at[half, 1], place.on_ring(axis, -1))
        second[half, 2] = copies.start(own_buf.at[half, here, 1, plus], tail_buf.at[half, 2], place.on_ring(axis, 1))
        second[half, 3] = copies.start(own_buf.at[half, here, 0, minus], tail_buf.at[half, 3], place.on_ring(axis, -1))
    for half in (0, 1):
        here = spots[half][0]
        axis = 1 - half
        _, plus, minus, _ = spots[axis]
        second[half, 0].wait_recv()
        own_buf[half, here, 0, plus] = own_buf[half, here, 0, plus] + tail_buf[half, 0]
        second[half, 4] = copies.start(own_buf.at[half, here, 0, plus], tail_buf.at[half, 4], place.on_ring(axis, 1))
        second[half, 1].wait_recv()
        own_buf[half, here, 1, minus] = own_buf[half, here, 1, minus] + tail_buf[half, 1]
        second[half, 5] = copies.start(own_buf.at[half, here, 1, minus], tail_buf.at[half, 5], place.on_ring(axis, -1))
    for half in (0, 1):
        here = spots[half][0]
        mine = spots[1 - half][0]
        cols = slice(half * half_cols, (half + 1) * half_cols)
        for slot in (2, 3, 4, 5):
            second[half, slot].wait_recv()
        sums[0, :, cols] = own_buf[half, here, 0, mine] + tail_buf[half, 3] + tail_buf[half, 4]
        sums[1, :, cols] = own_buf[half, here, 1, mine] + tail_buf[half, 2] + tail_buf[half, 5]


def all_gather(place, copies, fulls):
    core = place.core
    half_cols = fulls[0].shape[-1] // 2
    coords = (place.x, place.y)
    jobs = [(full, half) for full in fulls for half in (0, 1)]

    def piece(full, half, spot, other, micro):
        yy, xx = (other, spot) if half == 0 else (spot, other)
        cols = pl.ds(half * half_cols, half_cols)
        if micro is None:
            return full.at[:, core, yy, xx, :, cols]
        return full.at[micro, core, yy, xx, :, cols]

    def line(full, half, other):
        cols = pl.ds(half * half_cols, half_cols)
        if half == 0:
            return full.at[:, core, other, :, :, cols]
        return full.at[:, core, :, other, :, cols]

    def send(full, half, spot, other, micro, axis, by):
        ref = piece(full, half, spot, other, micro)
        return copies.start(ref, ref, place.on_ring(axis, by))

    def send_line(full, half, other):
        ref = line(full, half, other)
        return copies.start(ref, ref, place.partner)

    first, second, last = {}, {}, []
    for j, (full, half) in enumerate(jobs):
        spot, other = coords[half], coords[1 - half]
        for by in (1, -1):
            first[j, by] = send(full, half, spot, other, None, half, by)
        for by in (1, -1):
            second[j, 0, by] = send(full, half, spot, other, None, 1 - half, by)
    for j, (full, half) in enumerate(jobs):
        spot, other = coords[half], coords[1 - half]
        for by, micro in ((1, 0), (-1, 1)):
            first[j, by].wait_recv()
            came = place.shift(spot, -by)
            first[j, by, 'far'] = send(full, half, came, other, micro, half, by)
            for to in (1, -1):
                second[j, -by, to] = send(full, half, came, other, None, 1 - half, to)
    for j, (full, half) in enumerate(jobs):
        spot, other = coords[half], coords[1 - half]
        for by in (1, -1):
            first[j, by, 'far'].wait_recv()
        far = place.shift(spot, 2)
        for to in (1, -1):
            second[j, 2, to] = send(full, half, far, other, None, 1 - half, to)
        last.append(send_line(full, half, other))
    tails = {}
    for off in (0, 1, -1, 2):
        for j, (full, half) in enumerate(jobs):
            spot, other = coords[half], coords[1 - half]
            for to, micro in ((1, 0), (-1, 1)):
                second[j, off, to].wait_recv()
                came = place.shift(other, -to)
                tails[j, off, to] = send(full, half, place.shift(spot, off), came, micro, 1 - half, to)
    for j, (full, half) in enumerate(jobs):
        for to in (1, -1):
            last.append(send_line(full, half, place.shift(coords[1 - half], to)))
    for j, (full, half) in enumerate(jobs):
        for off in (0, 1, -1, 2):
            for to in (1, -1):
                tails[j, off, to].wait_recv()
        last.append(send_line(full, half, place.shift(coords[1 - half], 2)))
    for copy in last:
        copy.wait_recv()


def all_reduce(place, copies, value, pair_buf, ring_bufs, out):
    side = place.side
    copy = copies.start(value, pair_buf, place.partner)
    copy.wait_recv()
    total = value[...] + pair_buf[...]
    for axis in (0, 1):
        coord = place.x if axis == 0 else place.y
        buf = ring_bufs.at[axis]
        buf[coord] = total
        going = [copies.start(buf.at[coord], buf.at[coord], place.on_ring(axis, by)) for by in (1, -1, 2)]
        for copy in going:
            copy.wait_recv()
        total = buf[0]
        for k in range(1, side):
            total = total + buf[k]
    out[...] = total


def epilogue_forward(sums, residual, gain):
    row_sum = residual[...].astype(F32) + sums[...].astype(B16).astype(F32)
    new_rows = row_sum.astype(B16)
    normed = rms_scale(new_rows.astype(F32), gain[...].reshape(1, 1, -1)).astype(B16)
    return new_rows, normed


def epilogue_backward(sums, rows_in, gain, cot):
    vals = rows_in[...].astype(F32)
    grad = sums[...].astype(B16).astype(F32)
    inv = lax.rsqrt(jnp.mean(vals * vals, axis=-1, keepdims=True) + NORM_EPS)
    unit = vals * inv
    scaled = grad * gain[...].reshape(1, 1, -1)
    back = inv * (scaled - unit * jnp.mean(scaled * unit, axis=-1, keepdims=True))
    new_cot = (cot[...].astype(F32) + back).astype(B16)
    return new_cot, jnp.sum(jnp.sum(grad * unit, axis=0), axis=0, keepdims=True)


def stage_call(side, cid, kind, left, right, transposed, row_ins, gain, extra, grads):
    micro, rows, width = row_ins[0].shape
    half_cols = width // 2
    shard = jax.ShapeDtypeStruct((micro, rows, width), B16)
    full = jax.ShapeDtypeStruct((micro, CORES, side, side, rows, width), B16)
    part = jax.ShapeDtypeStruct((1, width), F32)
    reduces = kind != 'norm'
    new_full = kind in ('norm', 'fwd', 'bwd')
    outs = {'norm': [shard], 'fwd': [shard, shard], 'fwd_last': [shard], 'bwd': [shard, part], 'bwd_last': [shard]}[kind]
    n_small = len(outs)
    n_full = len(extra) + new_full
    outs = outs + [full] * n_full
    total_reduce = kind == 'bwd_last'
    n_terms = len(grads) + 1
    if total_reduce:
        outs = outs + [jax.ShapeDtypeStruct((2 * CORES * CORES, width), F32)]
    scratch = []
    if reduces:
        piece = (2, side, micro, side, rows, half_cols)
        scratch += [pltpu.VMEM(piece, F32)] * 3
        scratch += [pltpu.VMEM((2, 6, side, rows, half_cols), F32), pltpu.VMEM((2, 6, rows, half_cols), F32),
                    pltpu.VMEM((micro, rows, width), F32)]
    if total_reduce:
        scratch += [pltpu.VMEM((8, width), F32), pltpu.VMEM((8, width), F32), pltpu.VMEM((2, side, 8, width), F32)]
    n_sems = 48 * n_full + (32 if reduces else 0) + (7 if total_reduce else 0)
    scratch += [pltpu.SemaphoreType.DMA((n_sems,)), pltpu.SemaphoreType.DMA((n_sems,))]
    n_pair = len(left)
    n_rows, n_extra, n_grads = len(row_ins), len(extra), len(grads)
    has_gain = gain is not None

    def body(*refs):
        refs = list(refs)

        def take(count):
            got, refs[:] = refs[:count], refs[count:]
            return got
        lefts, rights, row_refs = take(n_pair), take(n_pair), take(n_rows)
        gain_ref = take(1)[0] if has_gain else None
        extra_refs, grad_refs = take(n_extra), take(n_grads)
        small_outs, full_outs = take(n_small), take(n_full)
        total_out = take(1)[0] if total_reduce else None
        if reduces:
            send_buf, own_buf, chip_buf, ring_buf, tail_buf, sums = take(6)
        if total_reduce:
            value, pair_buf, ring_bufs = take(3)
        send_sems, recv_sems = take(2)
        place = Place(side)
        copies = Copies(send_sems, recv_sems)
        entry_barrier(place, total_reduce)
        for ref, out in zip(extra_refs, full_outs):
            out[:, place.core, place.y, place.x] = ref[...]
        if reduces:
            pairs = list(zip(lefts, rights, [transposed] * n_pair))
            reduce_scatter(place, copies, pairs, send_buf, own_buf, chip_buf, ring_buf, tail_buf, sums, min(512, half_cols))
        new = None
        if kind == 'norm':
            new = rms_scale(row_refs[0][...].astype(F32), gain_ref[...].reshape(1, 1, -1)).astype(B16)
            small_outs[0][...] = new
        elif kind == 'fwd':
            new_rows, new = epilogue_forward(sums, row_refs[0], gain_ref)
            small_outs[0][...] = new_rows
            small_outs[1][...] = new
        elif kind == 'fwd_last':
            small_outs[0][...] = (row_refs[0][...].astype(F32) + sums[...].astype(B16).astype(F32)).astype(B16)
        else:
            new, gain_part = epilogue_backward(sums, row_refs[0], gain_ref, row_refs[1])
            small_outs[0][...] = new
            if total_reduce:
                value[...] = jnp.zeros_like(value)
                for i, ref in enumerate(grad_refs):
                    value[i:i + 1] = ref[...]
                value[n_terms - 1:n_terms] = gain_part
            else:
                small_outs[1][...] = gain_part
        if new_full:
            full_outs[-1][:, place.core, place.y, place.x] = new
        if full_outs:
            all_gather(place, copies, full_outs)
        if total_reduce:
            all_reduce(place, copies, value, pair_buf, ring_bufs, total_out)
        copies.finish()

    ins = list(left) + list(right) + list(row_ins) + ([gain.reshape(1, width)] if has_gain else []) + list(extra) + list(grads)
    vmem = pl.BlockSpec(memory_space=pltpu.VMEM)
    return pl.pallas_call(
        body, out_shape=outs, in_specs=[vmem] * len(ins), out_specs=[vmem] * len(outs), scratch_shapes=scratch,
        compiler_params=pltpu.CompilerParams(collective_id=cid, has_side_effects=True),
        name=f'stage_{kind}_{cid}')(*ins)


def attention_forward(queries, key_heads, value_heads, mask, score_scale):
    scores = jnp.einsum('mqe,mte->mqt', queries, key_heads, preferred_element_type=F32) * score_scale
    scores = jnp.where(mask, scores, -1e30)
    row_max = jnp.max(scores, axis=-1, keepdims=True)
    exp_scores = jnp.exp(scores - row_max)
    row_total = jnp.sum(exp_scores, axis=-1, keepdims=True)
    prob_b16 = (exp_scores / row_total).astype(B16)
    attn_mix = jnp.einsum('mqt,mte->mqe', prob_b16, value_heads, preferred_element_type=F32).astype(B16)
    return attn_mix, row_max + jnp.log(row_total)


def attention_backward(queries, key_heads, value_heads, log_norm, grad_mix, mask, score_scale):
    scores = jnp.einsum('mqe,mte->mqt', queries, key_heads, preferred_element_type=F32) * score_scale
    scores = jnp.where(mask, scores, -1e30)
    prob_f32 = jnp.exp(scores - log_norm)
    prob_b16 = prob_f32.astype(B16)
    grad_prob = jnp.einsum('mqe,mte->mqt', grad_mix, value_heads, preferred_element_type=F32).astype(B16).astype(F32)
    row_dot = jnp.sum(grad_prob * prob_f32, axis=-1, keepdims=True)
    grad_scores = (prob_f32 * (grad_prob - row_dot) * score_scale).astype(B16)
    grad_q = jnp.einsum('mqt,mte->mqe', grad_scores, key_heads, preferred_element_type=F32)
    grad_k = jnp.einsum('mqt,mqe->mte', grad_scores, queries, preferred_element_type=F32)
    grad_v = jnp.einsum('mqt,mqe->mte', prob_b16, grad_mix, preferred_element_type=F32)
    return grad_q, grad_k, grad_v


def solution(mesh):
    row_spec = P(None, ('dp', 'tp'), None)
    gain_spec = P(None, None)
    qkv_spec = P(None, None, 'tp', None, None)
    head_spec = P(None, 'tp', None, None)
    col_spec = P(None, None, 'tp')
    row_shard_spec = P(None, 'tp', None)
    side = math.isqrt(mesh.shape['tp'] // CORES)

    def device_program(x_in, y_cot, gain_attn, gain_mlp, w_qkv, w_out, w_gate, w_up, w_down):
        micro, rows, width = x_in.shape
        layer_count = w_qkv.shape[0]
        slots = w_qkv.shape[2] * w_qkv.shape[3]
        head_dim = w_qkv.shape[4]
        assert slots == 3 and side == 4 and micro == 2
        score_scale = head_dim ** -0.5
        seq = rows * side * side * CORES
        qkv_flat = w_qkv.reshape(layer_count, width, slots * head_dim)
        out_flat = w_out.reshape(layer_count, head_dim, width)
        pos = jnp.arange(seq, dtype=jnp.int32).reshape(side * side, CORES, rows).swapaxes(0, 1).reshape(seq)
        mask = (pos[:, None] >= pos[None, :])[None]
        call_ids = iter(range(64))

        def stage(kind, left=(), right=(), transposed=False, row_ins=(), gain=None, extra=(), grads=()):
            left = [item.reshape(micro, CORES, side * side * rows, item.shape[-1]) for item in left]
            return stage_call(side, next(call_ids), kind, left, list(right), transposed, list(row_ins), gain, list(extra), list(grads))

        def flat(full):
            return full.reshape(micro * seq, width)

        def dot(a, b, ca, cb):
            return lax.dot_general(a, b, (((ca,), (cb,)), ((), ())), preferred_element_type=F32)

        kept = []
        rows_x = x_in
        normed, full_u = stage('norm', row_ins=[x_in], gain=gain_attn[0])
        for layer in range(layer_count):
            qkv = dot(flat(full_u), qkv_flat[layer], 1, 0).astype(B16).reshape(micro, seq, slots * head_dim)
            queries, keys, values = (qkv[..., i * head_dim:(i + 1) * head_dim] for i in range(slots))
            attn_mix, log_norm = attention_forward(queries, keys, values, mask, score_scale)
            hidden, normed_b, full_v = stage('fwd', [attn_mix], [out_flat[layer]], False, [rows_x], gain_mlp[layer])
            gate_pre = dot(flat(full_v), w_gate[layer], 1, 0)
            up_proj = dot(flat(full_v), w_up[layer], 1, 0)
            inner = (jax.nn.silu(gate_pre) * up_proj).astype(B16)
            kept.append((rows_x, normed, hidden, normed_b, queries, keys, values, attn_mix, log_norm))
            if layer + 1 < layer_count:
                rows_x, normed, full_u = stage('fwd', [inner], [w_down[layer]], False, [hidden], gain_attn[layer + 1])
            else:
                rows_y, full_v, full_g = stage('fwd_last', [inner], [w_down[layer]], False, [hidden], None, [normed_b, y_cot])

        grad_rows = y_cot
        out_grads = [[None] * layer_count for _ in range(5)]
        gain_parts = {}
        for layer in reversed(range(layer_count)):
            rows_x, normed, hidden, normed_b, queries, keys, values, attn_mix, log_norm = kept[layer]
            flat_v, flat_g = flat(full_v), flat(full_g)
            gate_pre = dot(flat_v, w_gate[layer], 1, 0)
            up_proj = dot(flat_v, w_up[layer], 1, 0)
            gate_sig = jax.nn.sigmoid(gate_pre)
            gate_act = gate_pre * gate_sig
            inner = (gate_act * up_proj).astype(B16)
            out_grads[4][layer] = dot(inner, flat_g, 0, 0).astype(B16)
            grad_inner = dot(flat_g, w_down[layer], 1, 1).astype(B16).astype(F32)
            grad_up = (grad_inner * gate_act).astype(B16)
            grad_gate = (grad_inner * up_proj * gate_sig * (1.0 + gate_pre * (1.0 - gate_sig))).astype(B16)
            out_grads[2][layer] = dot(flat_v, grad_gate, 0, 0).astype(B16)
            out_grads[3][layer] = dot(flat_v, grad_up, 0, 0).astype(B16)
            grad_hidden, gain_parts['mlp', layer], full_u, full_gh = stage(
                'bwd', [grad_gate, grad_up], [w_gate[layer], w_up[layer]], True, [hidden, grad_rows], gain_mlp[layer], [normed])
            flat_u, flat_gh = flat(full_u), flat(full_gh)
            flat_mix = attn_mix.reshape(micro * seq, head_dim)
            out_grads[1][layer] = dot(flat_mix, flat_gh, 0, 0).astype(B16)
            grad_mix = dot(flat_gh, out_flat[layer], 1, 1).astype(B16).reshape(micro, seq, head_dim)
            grad_qkv = jnp.concatenate(attention_backward(queries, keys, values, log_norm, grad_mix, mask, score_scale), axis=-1).astype(B16)
            out_grads[0][layer] = dot(flat_u, grad_qkv.reshape(micro * seq, slots * head_dim), 0, 0).astype(B16)
            if layer > 0:
                grad_rows, gain_parts['attn', layer], full_v, full_g = stage(
                    'bwd', [grad_qkv], [qkv_flat[layer]], True, [rows_x, grad_hidden], gain_attn[layer], [kept[layer - 1][3]])
            else:
                terms = [gain_parts['attn', item] for item in range(1, layer_count)] + [gain_parts['mlp', item] for item in range(layer_count)]
                grad_rows, gain_sums = stage(
                    'bwd_last', [grad_qkv], [qkv_flat[layer]], True, [rows_x, grad_hidden], gain_attn[layer], [], terms)
        n_attn = layer_count - 1
        gain_a = jnp.concatenate([gain_sums[2 * layer_count - 1:2 * layer_count], gain_sums[:n_attn]], axis=0)
        gain_b = gain_sums[n_attn:n_attn + layer_count]
        return (rows_y, grad_rows,
                jnp.stack(out_grads[0]).reshape(w_qkv.shape), jnp.stack(out_grads[1]).reshape(w_out.shape),
                jnp.stack(out_grads[2]), jnp.stack(out_grads[3]), jnp.stack(out_grads[4]), gain_a, gain_b)

    return jax.shard_map(device_program, mesh=mesh,
                         in_specs=(row_spec, row_spec, gain_spec, gain_spec, qkv_spec, head_spec, col_spec, col_spec, row_shard_spec),
                         out_specs=(row_spec, row_spec, P('dp', None, 'tp', None, None), P('dp', 'tp', None, None), P('dp', None, 'tp'), P('dp', None, 'tp'), P('dp', 'tp', None), P('dp', None), P('dp', None)),
                         check_vma=False)
```

time: 1970 us -> 654 us (0.33)
  waiting for transfers between devices: 1690 us -> 0 us
  Pallas kernels: 0 us -> 522 us
  matrix products: 130 us -> 81.4 us
  blocking collectives: 46.4 us -> 0 us
  other arithmetic: 47.7 us -> 10.3 us
    reduce_scatter x16 -> x0, waiting for transfers between devices: 1120 us -> none  [the longest x4 293 us: device_program(): lax.psum_scatter(down_part, 'tp', scatter_dimension=0, tiled=True)]
    all_gather x16 -> x0, waiting for transfers between devices: 558 us -> none  [the longest x4 150 us: device_program(): normed_full = lax.all_gather(normed, 'tp', axis=0, tiled=True)]
    pallas_call x0 -> x9, Pallas kernels: none -> 522 us  [stage_call(): pl.pallas_call(body, out_shape=outs, in_specs=[vmem] * len(ins), out_spec...]
    psum x1 -> x0, blocking collectives: 46.4 us -> none  [device_program(): lax.psum(jnp.stack([jnp.stack(gain_a_acc), jnp.stack(gain_b_acc)]), 'tp')]
    dot_general x76 -> x36, matrix products: 116 us -> 81.4 us  [the longest x24 61.1 us: dot(): lax.dot_general(a, b, (((ca,), (cb,)), ((), ())), preferred_element_type=...]
  transfers between devices with their start and end apart: 32 -> 0, of which waited for: 32 -> 0; matrix products, arithmetic and copies ran while one was open for 7% -> 0% of each run, Pallas kernels for 0% -> 0%
where the time goes in v1:
time: 654 us; the launch traced here: 644 us
  Pallas kernels  522 us (80%)
  matrix products  81.4 us (12%)
  local copies, waits for them, and re-layouts  29 us (4%)
  other arithmetic  10.3 us (2%)
    pallas_call x9, Pallas kernels, stage_call(): pl.pallas_call(body, out_shape=outs, in_specs=[vmem] * len(ins), out_spec...  522 us
    dot_general x24, matrix products, dot(): lax.dot_general(a, b, (((ca,), (cb,)), ((), ())), preferred_element_type=...  61.1 us

profile of v1, /device:TPU:97, one launch (start us, length us, event | category | flops | bytes accessed | tf_op | source)
XLA Modules:
  0.0 644.2 jit_solution(11064841540125156245)
XLA Ops:
  3.8 2.0 slice_bitcast_fusion.6
  9.9 3.3 slice_bitcast_fusion
  13.2 2.1 slice_bitcast_fusion.4
  15.3 28.3 %stage_norm_0.1 = (bf16[2,16,2048]{2,1,0:T(8,128)(2,1)}, bf16[2,2,4,4,16,2048]{5,4,3,2,1,0:T(8,128)(2,1)}) custom-call(bf16[2,16,2048]{2,1,0:T(8,128)(2,1)} %refs_2_.3, f32[1,2048]{1,0:T(1,128)} %get-tuple-element.108.refs_1_.refs_4_), custom_call_target="tpu_custom_call" | custom-call | tf_op jit(solution)/shard_map/stage_norm_0/pallas_call | solution.py:371
  43.6 3.7 convolution_convert_fusion.15
  50.3 58.7 %stage_fwd_1.1 = (bf16[2,16,2048]{2,1,0:T(8,128)(2,1)}, bf16[2,16,2048]{2,1,0:T(8,128)(2,1)}, bf16[2,2,4,4,16,2048]{5,4,3,2,1,0:T(8,128)(2,1)}) custom-call(bf16[2,2,256,64]{3,2,1,0:T(8,128)(2,1)} %bitcast.166, bf16[64,2048]{1,0:T(8,128)(2,1)} %get-tuple-element.96.refs_1_, bf16[2,16,2048]{2,1,0:T(8,128)(2,1)} %refs_2_.3, ...), custom_call_target="tpu_custom_call" | custom-call | tf_op jit(solution)/shard_map/stage_fwd_1/pallas_call | solution.py:371
  109.0 3.9 fusion.103
  113.4 2.1 fusion.26
  115.4 57.0 %stage_fwd_2.1 = (bf16[2,16,2048]{2,1,0:T(8,128)(2,1)}, bf16[2,16,2048]{2,1,0:T(8,128)(2,1)}, bf16[2,2,4,4,16,2048]{5,4,3,2,1,0:T(8,128)(2,1)}) custom-call(bf16[2,2,256,256]{3,2,1,0:T(8,128)(2,1)} %bitcast.182, bf16[256,2048]{1,0:T(8,128)(2,1)} %get-tuple-element.88.refs_1_, bf16[2,16,2048]{2,1,0:T(8,128)(2,1)} %get-tuple-element.39.refs_2_.refs_4_, ...), custom_call_target="tpu_custom_call" | custom-call | tf_op jit(solution)/shard_map/stage_fwd_2/pallas_call | solution.py:371
  172.4 3.7 convolution_convert_fusion.14
  176.7 1.7 fusion.115
  180.6 59.0 %stage_fwd_3.1 = (bf16[2,16,2048]{2,1,0:T(8,128)(2,1)}, bf16[2,16,2048]{2,1,0:T(8,128)(2,1)}, bf16[2,2,4,4,16,2048]{5,4,3,2,1,0:T(8,128)(2,1)}) custom-call(bf16[2,2,256,64]{3,2,1,0:T(8,128)(2,1)} %bitcast.167, bf16[64,2048]{1,0:T(8,128)(2,1)} %get-tuple-element.95.refs_1_, bf16[2,16,2048]{2,1,0:T(8,128)(2,1)} %get-tuple-element.41.refs_2_, ...), custom_call_target="tpu_custom_call" | custom-call | tf_op jit(solution)/shard_map/stage_fwd_3/pallas_call | solution.py:371
  239.6 3.9 fusion.106
  244.0 2.1 fusion.27
  246.1 67.1 %stage_fwd_last_4.1 = (bf16[2,16,2048]{2,1,0:T(8,128)(2,1)}, bf16[2,2,4,4,16,2048]{5,4,3,2,1,0:T(8,128)(2,1)}, bf16[2,2,4,4,16,2048]{5,4,3,2,1,0:T(8,128)(2,1)}) custom-call(bf16[2,2,256,256]{3,2,1,0:T(8,128)(2,1)} %bitcast.183, bf16[256,2048]{1,0:T(8,128)(2,1)} %get-tuple-element.87.refs_1_, bf16[2,16,2048]{2,1,0:T(8,128)(2,1)} %get-tuple-element.43.refs_2_.refs_4_, ...), custom_call_target="tpu_custom_call" | custom-call | tf_op jit(solution)/shard_map/stage_fwd_last_4/pallas_call | solution.py:371
  313.2 3.9 fusion.105
  319.8 2.3 fusion.7
  323.7 2.4 fusion.5
  326.1 2.3 fusion.3
  328.4 68.1 %stage_bwd_5.1 = (bf16[2,16,2048]{2,1,0:T(8,128)(2,1)}, f32[1,2048]{1,0:T(1,128)}, bf16[2,2,4,4,16,2048]{5,4,3,2,1,0:T(8,128)(2,1)}, bf16[2,2,4,4,16,2048]{5,4,3,2,1,0:T(8,128)(2,1)}) custom-call(bf16[2,2,256,256]{3,2,1,0:T(8,128)(2,1)} %bitcast.173, bf16[2,2,256,256]{3,2,1,0:T(8,128)(2,1)} %bitcast.172, bf16[2048,256]{1,0:T(8,128)(2,1)} %get-tuple-element.113.refs_2_, ...), custom_call_target="tpu_custom_call" | custom-call | tf_op jit(solution)/shard_map/stage_bwd_5/pallas_call | solution.py:371
  396.5 3.9 fusion.9
  404.3 4.0 fusion.28
  408.3 4.0 fusion.29
  412.3 4.1 convolution_convert_fusion.6
  418.7 67.1 %stage_bwd_6.1 = (bf16[2,16,2048]{2,1,0:T(8,128)(2,1)}, f32[1,2048]{1,0:T(1,128)}, bf16[2,2,4,4,16,2048]{5,4,3,2,1,0:T(8,128)(2,1)}, bf16[2,2,4,4,16,2048]{5,4,3,2,1,0:T(8,128)(2,1)}) custom-call(bf16[2,2,256,192]{3,2,1,0:T(8,128)(2,1)} %pad_maximum_fusion.4.refs_0_, bf16[2048,192]{1,0:T(8,128)(2,1)} %copy.65.refs_1_, ...), custom_call_target="tpu_custom_call" | custom-call | tf_op jit(solution)/shard_map/stage_bwd_6/pallas_call | solution.py:371
  485.8 3.9 fusion.102
  503.0 67.8 %stage_bwd_7.1 = (bf16[2,16,2048]{2,1,0:T(8,128)(2,1)}, f32[1,2048]{1,0:T(1,128)}, bf16[2,2,4,4,16,2048]{5,4,3,2,1,0:T(8,128)(2,1)}, bf16[2,2,4,4,16,2048]{5,4,3,2,1,0:T(8,128)(2,1)}) custom-call(bf16[2,2,256,256]{3,2,1,0:T(8,128)(2,1)} %bitcast.171, bf16[2,2,256,256]{3,2,1,0:T(8,128)(2,1)} %bitcast.170, bf16[2048,256]{1,0:T(8,128)(2,1)} %get-tuple-element.114.refs_2_, ...), custom_call_target="tpu_custom_call" | custom-call | tf_op jit(solution)/shard_map/stage_bwd_7/pallas_call | solution.py:371
  570.8 3.2 fusion.8
  578.6 2.6 fusion.30
  581.3 2.6 fusion.31
  584.0 3.2 convolution_convert_fusion.7
  589.9 48.6 %stage_bwd_last_8.1 = (bf16[2,16,2048]{2,1,0:T(8,128)(2,1)}, f32[8,2048]{1,0:T(8,128)}) custom-call(bf16[2,2,256,192]{3,2,1,0:T(8,128)(2,1)} %pad_maximum_fusion.5.refs_0_, bf16[2048,192]{1,0:T(8,128)(2,1)} %copy.74.refs_1_, bf16[2,16,2048]{2,1,0:T(8,128)(2,1)} %refs_2_.3, bf16[2,16,2048]{2,1,0:T(8,128)(2,1)} %get-tuple-element.57.refs_3_, ...), custom_call_target="tpu_custom_call" | custom-call | tf_op jit(solution)/shard_map/stage_bwd_last_8/pallas_call | solution.py:371
  (144 shorter events, 49.8 us)
Async XLA Ops:
  3.8 44.1 %copy-start.27 = (pred[512,512]{0,1:T(8,128)(4,1)}, pred[512,512]{0,1:T(8,128)(4,1)S(1)}, u32[]{:S(2)}) copy-start(pred[512,512]{0,1:T(8,128)(4,1)S(1)} %broadcast_compare_fusion) | copy-start | bytes 786436
  9.9 3.3 copy-start.7
  9.9 3.3 copy-start.8
  109.0 3.9 copy-start.9
  109.0 4.4 copy-start.40
  176.7 2.1 copy-start.33
  176.7 2.1 copy-start.35
  176.7 2.1 copy-start.25
  239.6 3.9 copy-start.10
  239.6 4.4 copy-start.41
  313.2 3.9 copy-start.11
  313.2 4.4 copy-start.37
  317.6 2.2 copy-start.39
  319.8 2.3 copy-start.5
  323.7 2.4 copy-start.20
  323.7 2.4 copy-start.21
  328.4 72.0 %copy-start.4 = (bf16[2,1,64,2048]{3,2,1,0:T(8,128)(2,1)S(1)}, bf16[2,1,64,2048]{3,2,1,0:T(8,128)(2,1)}, u32[]{:S(2)}) copy-start(bf16[2,1,64,2048]{3,2,1,0:T(8,128)(2,1)} %param.14) | copy-start | bytes 1572868
  396.5 3.9 copy-start.1
  400.4 1.6 copy-start.3
  402.8 5.4 copy-start.34
  408.2 4.1 copy-start.22
  485.8 3.9 copy-start.12
  485.8 4.4 copy-start.36
  490.2 2.2 copy-start.38
  494.0 1.6 copy-start.15
  495.6 1.7 copy-start.18
  495.6 3.0 copy-start.19
  570.8 3.5 copy-start
  576.5 2.1 copy-start.32
  577.2 4.1 copy-start.30
  583.9 3.3 copy-start.17
  588.5 53.0 %copy-start.28 = (bf16[2,16,2048]{2,1,0:T(8,128)(2,1)S(1)}, bf16[2,16,2048]{2,1,0:T(8,128)(2,1)}, u32[]{:S(2)}) copy-start(bf16[2,16,2048]{2,1,0:T(8,128)(2,1)} %get-tuple-element.124) | copy-start | bytes 393220
  (10 other events, 12.0 us)

commit v2 on v0

v2 whole, which is shorter than its diff:
```python
import functools
import math

import jax
import jax.numpy as jnp
from jax import lax
from jax.experimental import pallas as pl
from jax.experimental.pallas import tpu as pltpu
from jax.sharding import PartitionSpec as P

NORM_EPS = 1e-5
MESH = pl.DeviceIdType.MESH
CORES = 2
F32 = jnp.float32
B16 = jnp.bfloat16


def rms_scale(row_vals, gain_vec):
    return row_vals * lax.rsqrt(jnp.mean(row_vals * row_vals, axis=-1, keepdims=True) + NORM_EPS) * gain_vec


class Place:
    def __init__(self, side):
        me = lax.axis_index('tp')
        self.side = side
        self.core = lax.rem(me, CORES)
        chip = lax.div(me, CORES)
        self.x = lax.rem(chip, side)
        self.y = lax.div(chip, side)
        self.partner = self.dev(self.y, self.x, 1 - self.core)

    def dev(self, y, x, core):
        return {'tp': (y * self.side + x) * CORES + core}

    def shift(self, coord, by):
        return lax.rem(coord + by + self.side, self.side)

    def on_ring(self, axis, by):
        if axis == 0:
            return self.dev(self.y, self.shift(self.x, by), self.core)
        return self.dev(self.shift(self.y, by), self.x, self.core)


class Copies:
    def __init__(self, send_sems, recv_sems):
        self.send_sems = send_sems
        self.recv_sems = recv_sems
        self.started = []

    def start(self, src, dst, target):
        idx = len(self.started)
        copy = pltpu.make_async_remote_copy(src_ref=src, dst_ref=dst, send_sem=self.send_sems.at[idx],
                                            recv_sem=self.recv_sems.at[idx], device_id=target, device_id_type=MESH)
        copy.start()
        self.started.append(copy)
        return copy

    def finish(self):
        for copy in self.started:
            copy.wait_send()


def entry_barrier(place):
    targets = [place.partner] + [place.on_ring(axis, by) for axis in (0, 1) for by in (1, -1, 2)]
    barrier = pltpu.get_barrier_semaphore()
    for target in targets:
        pl.semaphore_signal(barrier, inc=1, device_id=target, device_id_type=MESH)
    return lambda: pl.semaphore_wait(barrier, len(targets))


def add_rows(dst, *terms):
    def body(i, carry):
        total = terms[0][i]
        for term in terms[1:]:
            total = total + term[i]
        dst[i] = total
        return carry
    lax.fori_loop(0, dst.shape[0], body, 0)


class ReduceScatter:
    def __init__(self, place, copies, pairs, m, send_buf, own_buf, chip_buf, ring_buf, tail_buf, sums):
        self.place, self.copies, self.pairs, self.m = place, copies, pairs, m
        self.send_buf, self.own_buf, self.chip_buf, self.ring_buf, self.tail_buf, self.sums = (
            ref.at[m] for ref in (send_buf, own_buf, chip_buf, ring_buf, tail_buf, sums))
        self.quarter = self.own_buf.shape[-1]
        self.rows = self.own_buf.shape[-2]
        self.spots = [(coord, place.shift(coord, 1), place.shift(coord, -1), place.shift(coord, 2))
                      for coord in (place.x, place.y)]
        self.chip_copies, self.first, self.second = {}, {}, {}

    def products(self, half, core, buf):
        side, rows, quarter = self.place.side, self.rows, self.quarter

        def one(sub, carry):
            cols = pl.ds(pl.multiple_of((half * 2 + sub) * quarter, quarter), quarter)
            total = None
            for a_ref, b_ref, transposed in self.pairs:
                left = a_ref[self.m, :, core].reshape(side * side * rows, a_ref.shape[-1])
                if transposed:
                    part = lax.dot_general(left, b_ref[cols, :], (((1,), (1,)), ((), ())), preferred_element_type=F32)
                else:
                    part = jnp.dot(left, b_ref[:, cols], preferred_element_type=F32)
                total = part if total is None else total + part
            total = total.reshape(side, side, rows, quarter)
            for yy in range(side):
                for xx in range(side):
                    first, second = (xx, yy) if half == 0 else (yy, xx)
                    buf[half, first, sub, second] = total[yy, xx]
            return carry
        lax.fori_loop(0, 2, one, 0)

    def p0(self, entered=None):
        for half in (0, 1):
            self.products(half, 1 - self.place.core, self.send_buf)
            if entered is not None and half == 0:
                entered()
            self.to_partner(half, 'far', self.spots[half][3])
        for half in (0, 1):
            here, plus, minus, far = self.spots[half]
            for name, spot in (('plus', plus), ('minus', minus), ('here', here)):
                self.to_partner(half, name, spot)

    def to_partner(self, half, name, spot):
        self.chip_copies[half, name] = self.copies.start(self.send_buf.at[half, spot], self.chip_buf.at[half, spot], self.place.partner)

    def p1(self):
        for half in (0, 1):
            self.products(half, self.place.core, self.own_buf)

    def join(self, half, name, spot):
        self.chip_copies[half, name].wait_recv()
        for sub in (0, 1):
            add_rows(self.own_buf.at[half, spot, sub], self.own_buf.at[half, spot, sub], self.chip_buf.at[half, spot, sub])

    def ring(self, half, slot, spot, sub, by):
        self.first[half, slot] = self.copies.start(self.own_buf.at[half, spot, sub], self.ring_buf.at[half, slot], self.place.on_ring(half, by))

    def tail(self, half, slot, spot, sub, by):
        here = self.spots[half][0]
        self.second[half, slot] = self.copies.start(self.own_buf.at[half, here, sub, spot], self.tail_buf.at[half, slot],
                                                    self.place.on_ring(1 - half, by))

    def p2(self):
        for half in (0, 1):
            far = self.spots[half][3]
            self.join(half, 'far', far)
            self.ring(half, 0, far, 0, 1)
            self.ring(half, 1, far, 1, -1)

    def p3(self):
        for half in (0, 1):
            here, plus, minus, far = self.spots[half]
            self.join(half, 'plus', plus)
            self.ring(half, 2, plus, 1, 1)
            self.join(half, 'minus', minus)
            self.ring(half, 3, minus, 0, -1)
        for half in (0, 1):
            self.join(half, 'here', self.spots[half][0])

    def p4(self):
        own, ring = self.own_buf, self.ring_buf
        for half in (0, 1):
            here, plus, minus, far = self.spots[half]
            self.first[half, 0].wait_recv()
            add_rows(own.at[half, plus, 0], own.at[half, plus, 0], ring.at[half, 0])
            self.ring(half, 4, plus, 0, 1)
            self.first[half, 1].wait_recv()
            add_rows(own.at[half, minus, 1], own.at[half, minus, 1], ring.at[half, 1])
            self.ring(half, 5, minus, 1, -1)

    def p5(self):
        own, ring = self.own_buf, self.ring_buf
        for half in (0, 1):
            here = self.spots[half][0]
            _, plus, minus, far = self.spots[1 - half]
            for slot in (2, 3, 4, 5):
                self.first[half, slot].wait_recv()
            add_rows(own.at[half, here, 0], own.at[half, here, 0], ring.at[half, 3], ring.at[half, 4])
            add_rows(own.at[half, here, 1], own.at[half, here, 1], ring.at[half, 2], ring.at[half, 5])
            self.tail(half, 0, far, 0, 1)
            self.tail(half, 1, far, 1, -1)
            self.tail(half, 2, plus, 1, 1)
            self.tail(half, 3, minus, 0, -1)

    def p6(self):
        own, tail = self.own_buf, self.tail_buf
        for half in (0, 1):
            here = self.spots[half][0]
            _, plus, minus, _ = self.spots[1 - half]
            self.second[half, 0].wait_recv()
            own[half, here, 0, plus] = own[half, here, 0, plus] + tail[half, 0]
            self.tail(half, 4, plus, 0, 1)
            self.second[half, 1].wait_recv()
            own[half, here, 1, minus] = own[half, here, 1, minus] + tail[half, 1]
            self.tail(half, 5, minus, 1, -1)

    def p7(self):
        own, tail, quarter = self.own_buf, self.tail_buf, self.quarter
        for half in (0, 1):
            here, mine = self.spots[half][0], self.spots[1 - half][0]
            for slot in (2, 3, 4, 5):
                self.second[half, slot].wait_recv()
            start = half * 2 * quarter
            self.sums[:, start:start + quarter] = own[half, here, 0, mine] + tail[half, 3] + tail[half, 4]
            self.sums[:, start + quarter:start + 2 * quarter] = own[half, here, 1, mine] + tail[half, 2] + tail[half, 5]


class AllGather:
    def __init__(self, place, copies, arrays):
        self.place, self.copies = place, copies
        self.coords = (place.x, place.y)
        self.jobs = [(array, half) for array in arrays for half in (0, 1)]
        self.first, self.second, self.tails, self.last = {}, {}, {}, []

    def send(self, job, spot, other, sub, axis, by):
        array, half = job
        yy, xx = (other, spot) if half == 0 else (spot, other)
        half_cols = array.shape[-1] // 2
        cols = pl.ds(half * half_cols, half_cols) if sub is None else pl.ds(half * half_cols + sub * half_cols // 2, half_cols // 2)
        ref = array.at[yy, xx, self.place.core, :, cols]
        return self.copies.start(ref, ref, self.place.on_ring(axis, by))

    def send_line(self, job, other):
        array, half = job
        half_cols = array.shape[-1] // 2
        cols = pl.ds(half * half_cols, half_cols)
        core = self.place.core
        ref = array.at[other, :, core, :, cols] if half == 0 else array.at[:, other, core, :, cols]
        self.last.append(self.copies.start(ref, ref, self.place.partner))

    def each(self):
        for j, job in enumerate(self.jobs):
            half = job[1]
            yield j, job, half, self.coords[half], self.coords[1 - half]

    def a0(self):
        for j, job, half, spot, other in self.each():
            for by in (1, -1, 2):
                self.first[j, by] = self.send(job, spot, other, None, half, by)
            for by in (1, -1):
                self.second[j, 0, by] = self.send(job, spot, other, None, 1 - half, by)

    def a1(self):
        for j, job, half, spot, other in self.each():
            for by in (1, -1):
                self.first[j, by].wait_recv()
                came = self.place.shift(spot, -by)
                for to in (1, -1):
                    self.second[j, -by, to] = self.send(job, came, other, None, 1 - half, to)

    def a2(self):
        for j, job, half, spot, other in self.each():
            self.first[j, 2].wait_recv()
            far = self.place.shift(spot, 2)
            for to in (1, -1):
                self.second[j, 2, to] = self.send(job, far, other, None, 1 - half, to)
            self.send_line(job, other)

    def a3(self):
        for off in (0, 1, -1):
            self.pass_on(off)

    def pass_on(self, off):
        for j, job, half, spot, other in self.each():
            for to, sub in ((1, 0), (-1, 1)):
                self.second[j, off, to].wait_recv()
                came = self.place.shift(other, -to)
                self.tails[j, off, to] = self.send(job, self.place.shift(spot, off), came, sub, 1 - half, to)

    def a4(self):
        self.pass_on(2)
        for j, job, half, spot, other in self.each():
            for to in (1, -1):
                self.send_line(job, self.place.shift(other, to))

    def a5(self):
        for j, job, half, spot, other in self.each():
            for off in (0, 1, -1, 2):
                for to in (1, -1):
                    self.tails[j, off, to].wait_recv()
            self.send_line(job, self.place.shift(other, 2))

    def a6(self):
        for copy in self.last:
            copy.wait_recv()


def all_reduce(place, copies, value, pair_buf, ring_bufs, out):
    side = place.side
    copy = copies.start(value, pair_buf, place.partner)
    copy.wait_recv()
    total = value[...] + pair_buf[...]
    for axis in (0, 1):
        coord = place.x if axis == 0 else place.y
        buf = ring_bufs.at[axis]
        buf[coord] = total
        going = [copies.start(buf.at[coord], buf.at[coord], place.on_ring(axis, by)) for by in (1, -1, 2)]
        for copy in going:
            copy.wait_recv()
        total = buf[0]
        for k in range(1, side):
            total = total + buf[k]
    out[...] = total


def epilogue_forward(sums, residual, gain):
    new_rows = (residual.astype(F32) + sums.astype(B16).astype(F32)).astype(B16)
    return new_rows, rms_scale(new_rows.astype(F32), gain).astype(B16)


def epilogue_backward(sums, rows_in, gain, cot):
    vals = rows_in.astype(F32)
    grad = sums.astype(B16).astype(F32)
    inv = lax.rsqrt(jnp.mean(vals * vals, axis=-1, keepdims=True) + NORM_EPS)
    unit = vals * inv
    scaled = grad * gain
    back = inv * (scaled - unit * jnp.mean(scaled * unit, axis=-1, keepdims=True))
    new_cot = (cot.astype(F32) + back).astype(B16)
    return new_cot, jnp.sum(grad * unit, axis=0, keepdims=True)


def mm(a, b, ca, cb):
    return lax.dot_general(a, b, (((ca,), (cb,)), ((), ())), preferred_element_type=F32)


def rows_of(full, m):
    got = full[m]
    return got.reshape(-1, got.shape[-1])


def causal(scores, start):
    row = lax.broadcasted_iota(jnp.int32, scores.shape, 0) + start
    col = lax.broadcasted_iota(jnp.int32, scores.shape, 1)
    return jnp.where(row >= col, scores, -1e30)


def attention_forward(m, full, w_qkv, outs, scale, block):
    q_out, k_out, v_out, o_out, norm_out = outs
    rows = rows_of(full, m)
    for i, out in enumerate((q_out, k_out, v_out)):
        out[m] = mm(rows, w_qkv[i], 1, 1).astype(B16)
    for start in range(0, rows.shape[0], block):
        stop = start + block
        scores = causal(mm(q_out[m, start:stop], k_out[m, :stop], 1, 1) * scale, start)
        row_max = jnp.max(scores, axis=-1, keepdims=True)
        exp_scores = jnp.exp(scores - row_max)
        row_total = jnp.sum(exp_scores, axis=-1, keepdims=True)
        prob = (exp_scores / row_total).astype(B16)
        o_out[m, start:stop] = mm(prob, v_out[m, :stop], 1, 0).astype(B16)
        norm_out[m, start:stop] = jnp.broadcast_to(row_max + jnp.log(row_total), (block, norm_out.shape[-1]))


def attention_backward(m, full_g, w_out, kept, outs, mix_buf, acc, scale, block):
    q_in, k_in, v_in, o_in, norm_in = kept
    dq_out, dk_out, dv_out = outs
    mix_buf[...] = mm(rows_of(full_g, m), w_out[...], 1, 1).astype(B16)
    seq = mix_buf.shape[0]
    acc[...] = jnp.zeros_like(acc)
    for start in range(0, seq, block):
        stop = start + block
        queries, mix = q_in[m, start:stop], mix_buf[start:stop]
        keys = k_in[m, :stop]
        scores = causal(mm(queries, keys, 1, 1) * scale, start)
        prob = jnp.exp(scores - norm_in[m, start:stop, :1])
        grad_prob = mm(mix, v_in[m, :stop], 1, 1).astype(B16).astype(F32)
        row_dot = jnp.sum(grad_prob * prob, axis=-1, keepdims=True)
        grad_scores = (prob * (grad_prob - row_dot) * scale).astype(B16)
        dq_out[m, start:stop] = mm(grad_scores, keys, 1, 0).astype(B16)
        acc[0, :stop] += mm(grad_scores, queries, 0, 0)
        acc[1, :stop] += mm(prob.astype(B16), mix, 0, 0)
    dk_out[m] = acc[0].astype(B16)
    dv_out[m] = acc[1].astype(B16)


def mlp_forward(m, full, w_gate, w_up, out, block):
    rows = rows_of(full, m)
    for start in range(0, rows.shape[0], block):
        part = rows[start:start + block]
        gate = mm(part, w_gate[...], 1, 0)
        up = mm(part, w_up[...], 1, 0)
        out[m, start:start + block] = (gate * lax.logistic(gate) * up).astype(B16)


def mlp_backward(m, full_v, full_g, w_gate, w_up, w_down, dgate_out, dup_out, inner_buf, block):
    rows, grads = rows_of(full_v, m), rows_of(full_g, m)
    for start in range(0, rows.shape[0], block):
        part = rows[start:start + block]
        gate = mm(part, w_gate[...], 1, 0)
        up = mm(part, w_up[...], 1, 0)
        sig = lax.logistic(gate)
        act = gate * sig
        inner_buf[start:start + block] = (act * up).astype(B16)
        grad_inner = mm(grads[start:start + block], w_down[...], 1, 1).astype(B16).astype(F32)
        dup_out[m, start:start + block] = (grad_inner * act).astype(B16)
        dgate_out[m, start:start + block] = (grad_inner * up * sig * (1.0 + gate * (1.0 - sig))).astype(B16)


def weight_grad(m, left, right, acc, out, at, block):
    for start in range(0, right.shape[1], block):
        part = mm(left, right[:, start:start + block], 0, 0)
        cols = slice(start, start + block)
        if m == 0:
            acc[:, cols] = part
        else:
            total = (acc[:, cols] + part).astype(B16)
            if at is None:
                out[:, cols] = total
            else:
                out[at, :, cols] = total


def weight_grad_rows(m, left, right, acc, out, block):
    for start in range(0, left.shape[1], block):
        part = mm(left[:, start:start + block], right, 0, 0)
        if m == 0:
            acc[start:start + block] = part
        else:
            out[start:start + block] = (acc[start:start + block] + part).astype(B16)


def stage_call(side, cid, kind, post, left, right, layer, transposed, row_ins, gain, extra, grads, weights, kept, scale):
    micro, rows, width = row_ins[0].shape
    quarter = width // 4
    seq = side * side * CORES * rows
    sds = jax.ShapeDtypeStruct
    shard = sds((micro, rows, width), B16)
    part = sds((1, width), F32)
    reduces = kind != 'norm'
    new_full = kind in ('norm', 'fwd', 'bwd')
    outs = {'norm': [shard], 'fwd': [shard, shard], 'fwd_last': [shard], 'bwd': [shard, part], 'bwd_last': [shard]}[kind]
    n_small = len(outs)
    n_full = len(extra) + new_full
    total_reduce = kind == 'bwd_last'
    n_terms = len(grads) + 1
    if total_reduce:
        outs = outs + [sds((8, width), F32)]
    post_outs, post_scratch = [], []
    head = weights[0].shape[-2] if post in ('attn', 'attn_bwd') else 0
    if post == 'attn':
        post_outs = [sds((micro, seq, head), B16)] * 4 + [sds((micro, seq, 128), F32)]
    elif post == 'mlp':
        post_outs = [sds((micro, seq, weights[0].shape[-1]), B16)]
    elif post == 'attn_bwd':
        post_outs = [sds((micro, seq, head), B16)] * 3 + [sds((head, width), B16), sds((3, head, width), B16)]
        post_scratch = [pltpu.VMEM((seq, head), B16), pltpu.VMEM((2, seq, head), F32), pltpu.VMEM((head, width), F32), pltpu.VMEM((3, head, width), F32)]
    elif post == 'mlp_bwd':
        ff = weights[0].shape[-1]
        post_outs = [sds((micro, seq, ff), B16)] * 2 + [sds((width, ff), B16)] * 2 + [sds((ff, width), B16)]
        post_scratch = [pltpu.VMEM((seq, ff), B16), pltpu.VMEM((width, ff), F32), pltpu.VMEM((width, ff), F32), pltpu.VMEM((ff, width), F32)]
    outs = outs + post_outs
    scratch = [pltpu.VMEM((micro, side, side, CORES, rows, width), B16)] * n_full
    n_pair, n_weights = len(left), len(weights)
    if reduces:
        piece = (micro, 2, side, 2, side, rows, quarter)
        scratch += [pltpu.VMEM(piece, F32)] * 3
        scratch += [pltpu.VMEM((micro, 2, 6, side, rows, quarter), F32), pltpu.VMEM((micro, 2, 6, rows, quarter), F32),
                    pltpu.VMEM((micro, rows, width), F32)]
    scratch += [pltpu.VMEM(item.shape[1:], B16) for item in right + weights] + [pltpu.SemaphoreType.DMA((max(1, len(right) + n_weights),))]
    if total_reduce:
        scratch += [pltpu.VMEM((8, width), F32), pltpu.VMEM((8, width), F32), pltpu.VMEM((2, side, 8, width), F32)]
    n_sems = micro * (48 * n_full + (32 if reduces else 0)) + (7 if total_reduce else 0)
    scratch += post_scratch + [pltpu.SemaphoreType.DMA((n_sems,)), pltpu.SemaphoreType.DMA((n_sems,))]
    n_rows, n_extra, n_grads, n_right, n_kept = len(row_ins), len(extra), len(grads), len(right), len(kept)
    has_gain = gain is not None

    def body(*refs):
        refs = list(refs)

        def take(count):
            got, refs[:] = refs[:count], refs[count:]
            return got
        lefts, rights, row_refs = take(n_pair), take(n_right), take(n_rows)
        gain_ref = take(1)[0] if has_gain else None
        extra_refs, grad_refs, weight_refs, kept_refs = take(n_extra), take(n_grads), take(n_weights), take(n_kept)
        small_outs = take(n_small)
        total_out = take(1)[0] if total_reduce else None
        post_refs = take(len(post_outs))
        full_bufs = take(n_full)
        if reduces:
            send_buf, own_buf, chip_buf, ring_buf, tail_buf, sums = take(6)
        held = take(n_right + n_weights)
        weight_sems = take(1)[0]
        loads = []
        for i, ref in enumerate(rights + weight_refs):
            loads.append(pltpu.make_async_copy(ref.at[layer[0] if i < n_right else layer[1]], held[i], weight_sems.at[i]))
            loads[-1].start()
        product_weights, post_weights = held[:n_right], held[n_right:]
        if total_reduce:
            value, pair_buf, ring_bufs = take(3)
        work = take(len(post_scratch))
        send_sems, recv_sems = take(2)
        place = Place(side)
        copies = Copies(send_sems, recv_sems)
        entered = entry_barrier(place)
        for ref, out in zip(extra_refs, full_bufs):
            for m in range(micro):
                out[m, place.y, place.x, place.core] = ref[m]
        gain_parts = []

        def gather_new(m):
            gain_row = gain_ref[...] if has_gain else None
            new = None
            if kind == 'norm':
                new = rms_scale(row_refs[0][m].astype(F32), gain_row).astype(B16)
                small_outs[0][m] = new
            elif kind == 'fwd':
                small_outs[0][m], new = epilogue_forward(sums[m], row_refs[0][m], gain_row)
                small_outs[1][m] = new
            elif kind == 'fwd_last':
                small_outs[0][m] = (row_refs[0][m].astype(F32) + sums[m].astype(B16).astype(F32)).astype(B16)
            else:
                new, gain_part = epilogue_backward(sums[m], row_refs[0][m], gain_row, row_refs[1][m])
                small_outs[0][m] = new
                gain_parts.append(gain_part)
            if new_full:
                full_bufs[-1][m, place.y, place.x, place.core] = new

        def post_a(m):
            if m == 0:
                for load in loads[n_right:]:
                    load.wait()
            if post == 'attn':
                attention_forward(m, full_bufs[-1], post_weights[0], post_refs, scale, 128)
            elif post == 'mlp':
                mlp_forward(m, full_bufs[-1], post_weights[0], post_weights[1], post_refs[0], 256)
            elif post == 'attn_bwd':
                attention_backward(m, full_bufs[-1], post_weights[0], kept_refs, post_refs[:3], work[0], work[1], scale, 128)
            elif post == 'mlp_bwd':
                mlp_backward(m, full_bufs[0], full_bufs[-1], *post_weights, post_refs[0], post_refs[1], work[0], 256)

        def post_b(m):
            if post == 'attn_bwd':
                weight_grad(m, kept_refs[3][m], rows_of(full_bufs[-1], m), work[2], post_refs[3], None, 512)
                for i in range(3):
                    weight_grad(m, post_refs[i][m], rows_of(full_bufs[0], m), work[3].at[i], post_refs[4], i, 512)
            elif post == 'mlp_bwd':
                rows_v = rows_of(full_bufs[0], m)
                weight_grad_rows(m, rows_v, post_refs[0][m], work[1], post_refs[2], 512)
                weight_grad_rows(m, rows_v, post_refs[1][m], work[2], post_refs[3], 512)
                weight_grad(m, work[0][...], rows_of(full_bufs[-1], m), work[3], post_refs[4], None, 512)

        early = [AllGather(place, copies, [buf.at[m] for buf in full_bufs[:n_extra]]) for m in range(micro)]
        late = [AllGather(place, copies, [full_bufs[-1].at[m]] if new_full else []) for m in range(micro)]
        first_early = not new_full

        def early_step(name, when):
            if when == first_early:
                for job in early:
                    getattr(job, name)()
        if reduces:
            for load in loads[:n_right]:
                load.wait()
            pairs = [(a, b, transposed) for a, b in zip(lefts, [product_weights[0].at[i] for i in range(n_pair)] if n_pair > n_right else product_weights)]
            sum0, sum1 = (ReduceScatter(place, copies, pairs, m, send_buf, own_buf, chip_buf, ring_buf, tail_buf, sums)
                          for m in range(micro))
            sum0.p0(entered)
            early_step('a0', True)
            sum0.p1()
            sum0.p2()
            sum1.p0()
            sum0.p3()
            sum1.p1()
            sum1.p2()
            sum0.p4()
            sum1.p3()
            early_step('a1', True)
            sum0.p5()
            sum1.p4()
            sum0.p6()
            early_step('a2', True)
            early_step('a0', False)
            sum1.p5()
            sum0.p7()
        else:
            entered()
        gather_new(0)
        late[0].a0()
        if reduces:
            sum1.p6()
            late[0].a1()
            early_step('a1', False)
            early_step('a3', True)
            sum1.p7()
        gather_new(1)
        late[1].a0()
        if not reduces:
            late[0].a1()
        late[0].a2()
        early_step('a2', False)
        late[1].a1()
        late[0].a3()
        early_step('a3', False)
        late[1].a2()
        late[0].a4()
        late[1].a3()
        late[0].a5()
        late[1].a4()
        early[0].a4()
        late[0].a6()
        early_first = post == 'mlp_bwd'
        if not early_first:
            post_a(0)
        late[1].a5()
        early[1].a4()
        early[0].a5()
        early[0].a6()
        if early_first:
            post_a(0)
        early[1].a5()
        post_b(0)
        early[1].a6()
        late[1].a6()
        post_a(1)
        post_b(1)
        if total_reduce:
            value[...] = jnp.zeros_like(value)
            for i, ref in enumerate(grad_refs):
                value[i:i + 1] = ref[...]
            value[n_terms - 1:n_terms] = gain_parts[0] + gain_parts[1]
            all_reduce(place, copies, value, pair_buf, ring_bufs, total_out)
        elif gain_parts:
            small_outs[1][...] = gain_parts[0] + gain_parts[1]
        copies.finish()

    ins = list(left) + list(right) + list(row_ins) + ([gain.reshape(1, width)] if has_gain else []) + list(extra) + list(grads)
    vmem = pl.BlockSpec(memory_space=pltpu.VMEM)
    whole = pl.BlockSpec(memory_space=pl.ANY)
    in_specs = [vmem] * len(ins)
    in_specs[n_pair:n_pair + n_right] = [whole] * n_right
    in_specs += [whole] * n_weights + [vmem] * n_kept
    ins += list(weights) + list(kept)
    return pl.pallas_call(
        body, out_shape=outs, in_specs=in_specs, out_specs=[vmem] * len(outs), scratch_shapes=scratch,
        compiler_params=pltpu.CompilerParams(collective_id=cid, has_side_effects=True, vmem_limit_bytes=64 * 1024 * 1024 - 65536),
        name=f'stage_{kind}_{cid}')(*ins)


def solution(mesh):
    row_spec = P(None, ('dp', 'tp'), None)
    gain_spec = P(None, None)
    qkv_spec = P(None, None, 'tp', None, None)
    head_spec = P(None, 'tp', None, None)
    col_spec = P(None, None, 'tp')
    row_shard_spec = P(None, 'tp', None)
    side = math.isqrt(mesh.shape['tp'] // CORES)

    def device_program(x_in, y_cot, gain_attn, gain_mlp, w_qkv, w_out, w_gate, w_up, w_down):
        micro, rows, width = x_in.shape
        layer_count = w_qkv.shape[0]
        slots = w_qkv.shape[2] * w_qkv.shape[3]
        head_dim = w_qkv.shape[4]
        assert slots == 3 and side == 4 and micro == 2
        qkv_flat = w_qkv.transpose(0, 2, 3, 4, 1).reshape(layer_count, slots, head_dim, width)
        out_flat = w_out.reshape(layer_count, head_dim, width)
        call_ids = iter(range(64))

        def stage(kind, post=None, left=(), right=(), layer=(0, 0), transposed=False, row_ins=(), gain=None, extra=(), grads=(), weights=(), kept=()):
            left = [item.reshape(micro, side * side, CORES, rows, item.shape[-1]) for item in left]
            return stage_call(side, next(call_ids), kind, post, left, list(right), layer, transposed, list(row_ins), gain, list(extra),
                              list(grads), list(weights), list(kept), head_dim ** -0.5)

        kept = []
        rows_x = x_in
        normed, *attn = stage('norm', 'attn', layer=(0, 0), row_ins=[x_in], gain=gain_attn[0], weights=[qkv_flat])
        for layer in range(layer_count):
            hidden, normed_b, inner = stage('fwd', 'mlp', [attn[3]], [out_flat], (layer, layer), False, [rows_x], gain_mlp[layer],
                                            weights=[w_gate, w_up])
            kept.append((rows_x, normed, hidden, normed_b, attn))
            if layer + 1 < layer_count:
                rows_x, normed, *attn = stage('fwd', 'attn', [inner], [w_down], (layer, layer + 1), False, [hidden], gain_attn[layer + 1],
                                              weights=[qkv_flat])
            else:
                rows_y, *mlp = stage('fwd_last', 'mlp_bwd', [inner], [w_down], (layer, layer), False, [hidden], None, [normed_b, y_cot],
                                     weights=[w_gate, w_up, w_down])

        grad_rows = y_cot
        out_grads = [[None] * layer_count for _ in range(5)]
        gain_parts = {}
        for layer in reversed(range(layer_count)):
            rows_x, normed, hidden, normed_b, attn = kept[layer]
            grad_gate, grad_up, out_grads[2][layer], out_grads[3][layer], out_grads[4][layer] = mlp
            grad_hidden, gain_parts['mlp', layer], *grad_qkv, out_grads[1][layer], out_grads[0][layer] = stage(
                'bwd', 'attn_bwd', [grad_gate, grad_up], [w_gate, w_up], (layer, layer), True, [hidden, grad_rows], gain_mlp[layer], [normed],
                weights=[out_flat], kept=attn)
            if layer > 0:
                grad_rows, gain_parts['attn', layer], *mlp = stage(
                    'bwd', 'mlp_bwd', grad_qkv, [qkv_flat], (layer, layer - 1), False, [rows_x, grad_hidden], gain_attn[layer], [kept[layer - 1][3]],
                    weights=[w_gate, w_up, w_down])
            else:
                terms = [gain_parts['attn', item] for item in range(1, layer_count)] + [gain_parts['mlp', item] for item in range(layer_count)]
                grad_rows, gain_sums = stage(
                    'bwd_last', None, grad_qkv, [qkv_flat], (layer, layer), False, [rows_x, grad_hidden], gain_attn[layer], grads=terms)
        n_attn = layer_count - 1
        gain_a = jnp.concatenate([gain_sums[2 * layer_count - 1:2 * layer_count], gain_sums[:n_attn]], axis=0)
        gain_b = gain_sums[n_attn:n_attn + layer_count]
        return (rows_y, grad_rows,
                jnp.stack(out_grads[0]).reshape(layer_count, 1, slots, head_dim, width).transpose(0, 4, 1, 2, 3), jnp.stack(out_grads[1]).reshape(w_out.shape),
                jnp.stack(out_grads[2]), jnp.stack(out_grads[3]), jnp.stack(out_grads[4]), gain_a, gain_b)

    return jax.shard_map(device_program, mesh=mesh,
                         in_specs=(row_spec, row_spec, gain_spec, gain_spec, qkv_spec, head_spec, col_spec, col_spec, row_shard_spec),
                         out_specs=(row_spec, row_spec, P('dp', None, 'tp', None, None), P('dp', 'tp', None, None), P('dp', None, 'tp'), P('dp', None, 'tp'), P('dp', 'tp', None), P('dp', None), P('dp', None)),
                         check_vma=False)
```

time: 1970 us -> 550 us (0.28)
  waiting for transfers between devices: 1690 us -> 0 us
  Pallas kernels: 0 us -> 526 us
  matrix products: 130 us -> 0 us
  blocking collectives: 46.4 us -> 0 us
  other arithmetic: 47.7 us -> 9.18 us
  local copies, waits for them, and re-layouts: 33.1 us -> 7.92 us
    reduce_scatter x16 -> x0, waiting for transfers between devices: 1120 us -> none  [the longest x4 293 us: device_program(): lax.psum_scatter(down_part, 'tp', scatter_dimension=0, tiled=True)]
    all_gather x16 -> x0, waiting for transfers between devices: 558 us -> none  [the longest x4 150 us: device_program(): normed_full = lax.all_gather(normed, 'tp', axis=0, tiled=True)]
    pallas_call x0 -> x9, Pallas kernels: none -> 526 us  [stage_call(): pl.pallas_call(body, out_shape=outs, in_specs=in_specs, out_specs=[vmem]...]
    dot_general x76 -> x0, matrix products: 116 us -> none  [the longest x4 13.9 us: device_program(): jnp.einsum('sd,fd->sf', grad_full, w_down[layer_idx], preferred_element_t...]
    psum x1 -> x0, blocking collectives: 46.4 us -> none  [device_program(): lax.psum(jnp.stack([jnp.stack(gain_a_acc), jnp.stack(gain_b_acc)]), 'tp')]
    unnamed x320 -> x18, local copies, waits for them, and re-layouts: 27.1 us -> 2.73 us
  transfers between devices with their start and end apart: 32 -> 0, of which waited for: 32 -> 0; matrix products, arithmetic and copies ran while one was open for 7% -> 0% of each run, Pallas kernels for 0% -> 0%
where the time goes in v2:
time: 550 us; the launch traced here: 544 us
  Pallas kernels  526 us (96%)
  other arithmetic  9.18 us (2%)
  local copies, waits for them, and re-layouts  7.92 us (1%)
    pallas_call x9, Pallas kernels, stage_call(): pl.pallas_call(body, out_shape=outs, in_specs=in_specs, out_specs=[vmem]...  526 us

profile of v2, /device:TPU:97, one launch (start us, length us, event | category | flops | bytes accessed | tf_op | source)
XLA Modules:
  0.0 544.4 jit_solution(6637110006817755444)
XLA Ops:
  0.6 1.4 fusion.2
  2.0 1.4 fusion.1
  3.5 33.4 %stage_norm_0.1 = (bf16[2,16,2048]{2,1,0:T(8,128)(2,1)}, bf16[2,512,64]{2,1,0:T(8,128)(2,1)}, bf16[2,512,64]{2,1,0:T(8,128)(2,1)}, bf16[2,512,64]{2,1,0:T(8,128)...) custom-call(bf16[2,16,2048]{2,1,0:T(8,128)(2,1)} %refs_4_.7, f32[1,2048]{1,0:T(1,128)} %get-tuple-element.119.refs_1_.refs_6_, ...), custom_call_target="tpu_custom_call" | custom-call | tf_op jit(solution)/shard_map/stage_norm_0/pallas_call | solution.py:633
  36.8 53.8 %stage_fwd_1.1 = (bf16[2,16,2048]{2,1,0:T(8,128)(2,1)}, bf16[2,16,2048]{2,1,0:T(8,128)(2,1)}, bf16[2,512,256]{2,1,0:T(8,128)(2,1)}) custom-call(bf16[2,16,2,16,64]{4,3,2,1,0:T(8,128)(2,1)} %bitcast.48, bf16[2,64,2048]{2,1,0:T(8,128)(2,1)} %bitcast.44, bf16[2,16,2048]{2,1,0:T(8,128)(2,1)} %refs_4_.7, f32[1,2048]{1,0:T(1,128)} %get-tuple-element.117.refs_3_.refs_6_, ...), custom_call_target="tpu_custom_call" | custom-call | tf_op jit(solution)/shard_map/stage_fwd_1/pallas_call | solution.py:633
  90.6 56.8 %stage_fwd_2.1 = (bf16[2,16,2048]{2,1,0:T(8,128)(2,1)}, bf16[2,16,2048]{2,1,0:T(8,128)(2,1)}, bf16[2,512,64]{2,1,0:T(8,128)(2,1)}, bf16[2,512,64]{2,1,0:T(8,128)...) custom-call(bf16[2,16,2,16,256]{4,3,2,1,0:T(8,128)(2,1)} %bitcast.62, ...), custom_call_target="tpu_custom_call" | custom-call | tf_op jit(solution)/shard_map/stage_fwd_2/pallas_call | solution.py:633
  147.4 54.1 %stage_fwd_3.1 = (bf16[2,16,2048]{2,1,0:T(8,128)(2,1)}, bf16[2,16,2048]{2,1,0:T(8,128)(2,1)}, bf16[2,512,256]{2,1,0:T(8,128)(2,1)}) custom-call(bf16[2,16,2,16,64]{4,3,2,1,0:T(8,128)(2,1)} %bitcast.49, bf16[2,64,2048]{2,1,0:T(8,128)(2,1)} %bitcast.45, bf16[2,16,2048]{2,1,0:T(8,128)(2,1)} %get-tuple-element.61.refs_2_.refs_4_, ...), custom_call_target="tpu_custom_call" | custom-call | tf_op jit(solution)/shard_map/stage_fwd_3/pallas_call | solution.py:633
  201.5 66.6 %stage_fwd_last_4.1 = (bf16[2,16,2048]{2,1,0:T(8,128)(2,1)}, bf16[2,512,256]{2,1,0:T(8,128)(2,1)}, bf16[2,512,256]{2,1,0:T(8,128)(2,1)}, bf16[2048,256]{1,0:T(8,...) custom-call(bf16[2,16,2,16,256]{4,3,2,1,0:T(8,128)(2,1)} %bitcast.63, bf16[2,256,2048]{2,1,0:T(8,128)(2,1)} %refs_10_.1, ...), custom_call_target="tpu_custom_call" | custom-call | tf_op jit(solution)/shard_map/stage_fwd_last_4/pallas_call | solution.py:633
  268.2 71.5 %stage_bwd_5.1 = (bf16[2,16,2048]{2,1,0:T(8,128)(2,1)}, f32[1,2048]{1,0:T(1,128)}, bf16[2,512,64]{2,1,0:T(8,128)(2,1)}, bf16[2,512,64]{2,1,0:T(8,128)(2,1)}, bf1...) custom-call(bf16[2,16,2,16,256]{4,3,2,1,0:T(8,128)(2,1)} %bitcast.60, ...), custom_call_target="tpu_custom_call" | custom-call | tf_op jit(solution)/shard_map/stage_bwd_5/pallas_call | solution.py:633
  339.7 70.6 %stage_bwd_6.1 = (bf16[2,16,2048]{2,1,0:T(8,128)(2,1)}, f32[1,2048]{1,0:T(1,128)}, bf16[2,512,256]{2,1,0:T(8,128)(2,1)}, bf16[2,512,256]{2,1,0:T(8,128)(2,1)}, b...) custom-call(bf16[2,16,2,16,64]{4,3,2,1,0:T(8,128)(2,1)} %bitcast.64, ...), custom_call_target="tpu_custom_call" | custom-call | tf_op jit(solution)/shard_map/stage_bwd_6/pallas_call | solution.py:633
  410.4 72.5 %stage_bwd_7.1 = (bf16[2,16,2048]{2,1,0:T(8,128)(2,1)}, f32[1,2048]{1,0:T(1,128)}, bf16[2,512,64]{2,1,0:T(8,128)(2,1)}, bf16[2,512,64]{2,1,0:T(8,128)(2,1)}, bf1...) custom-call(bf16[2,16,2,16,256]{4,3,2,1,0:T(8,128)(2,1)} %bitcast.58, ...), custom_call_target="tpu_custom_call" | custom-call | tf_op jit(solution)/shard_map/stage_bwd_7/pallas_call | solution.py:633
  482.9 46.8 %stage_bwd_last_8.1 = (bf16[2,16,2048]{2,1,0:T(8,128)(2,1)}, f32[8,2048]{1,0:T(8,128)}) custom-call(bf16[2,16,2,16,64]{4,3,2,1,0:T(8,128)(2,1)} %bitcast.69, bf16[2,16,2,16,64]{4,3,2,1,0:T(8,128)(2,1)} %bitcast.70, bf16[2,16,2,16,64]{4,3,2,1,0:T(8,128)(2,1)} %bitcast.71, bf16[2,3,64,2048]{3,2,1,0:T(8,128)(2,1)} %bitcast.43, bf16[2,16,2048]{2,1,0:T(8,128)(2,1)} %refs_4_.7, ...), custom_call_target="tpu_custom_call" | custom-call | tf_op jit(solution)/shard_map/stage_bwd_last_8/pallas_call | solution.py:633
  529.7 1.5 slice.31
  531.2 0.9 fusion
  532.1 0.6 pad_maximum_fusion.3
  532.7 0.0 copy-start
  532.7 2.0 maximum_bitcast_fusion.1
  534.7 2.7 maximum_bitcast_fusion
  537.4 0.0 copy-done
  537.4 0.0 copy-done.1
  537.4 0.0 copy-start.3
  537.4 0.0 copy-start.4
  537.4 0.0 copy-start.5
  537.4 1.5 pad_maximum_fusion.2
  538.9 0.0 copy-done.2
  538.9 0.8 copy-done.3
  539.7 0.3 copy-done.4
  540.0 0.3 copy-done.5
  540.3 2.4 pad_maximum_fusion
  542.7 0.0 copy-done.6
  542.7 0.7 copy.23
  543.4 0.0 copy-done.7
  543.4 0.7 copy.24
  (4 shorter events, 0.0 us)
Async XLA Ops:
  532.7 4.7 copy-start
  532.7 4.7 copy-start.1
  537.4 1.5 copy-start.2
  537.4 2.3 copy-start.3
  537.4 2.6 copy-start.4
  537.4 2.9 copy-start.5
  540.3 2.4 copy-start.6
  540.3 3.0 copy-start.7

commit v3 on v2

--- a/solution.py
+++ b/solution.py
@@ -45,19 +45,31 @@
     def __init__(self, send_sems, recv_sems):
         self.send_sems = send_sems
         self.recv_sems = recv_sems
-        self.started = []
-
-    def start(self, src, dst, target):
-        idx = len(self.started)
-        copy = pltpu.make_async_remote_copy(src_ref=src, dst_ref=dst, send_sem=self.send_sems.at[idx],
-                                            recv_sem=self.recv_sems.at[idx], device_id=target, device_id_type=MESH)
+        self.send_groups, self.recv_groups = {}, {}
+        self.recv_count = 0
+
+    def start(self, src, dst, target, group, total, recv_group=None):
+        if group not in self.send_groups:
+            self.send_groups[group] = (len(self.send_groups), total)
+        if recv_group is None:
+            recv_idx = self.recv_count
+            self.recv_count += 1
+        else:
+            if recv_group not in self.recv_groups:
+                self.recv_groups[recv_group] = self.recv_count
+                self.recv_count += 1
+            recv_idx = self.recv_groups[recv_group]
+        copy = pltpu.make_async_remote_copy(src_ref=src, dst_ref=dst, send_sem=self.send_sems.at[self.send_groups[group][0]],
+                                            recv_sem=self.recv_sems.at[recv_idx], device_id=target, device_id_type=MESH)
         copy.start()
-        self.started.append(copy)
         return copy
 
+    def wait_group(self, recv_group, total):
+        pltpu.make_async_copy(total, total, self.recv_sems.at[self.recv_groups[recv_group]]).wait()
+
     def finish(self):
-        for copy in self.started:
-            copy.wait_send()
+        for idx, total in self.send_groups.values():
+            pltpu.make_async_copy(total, total, self.send_sems.at[idx]).wait()
 
 
 def entry_barrier(place):
@@ -122,7 +134,8 @@
                 self.to_partner(half, name, spot)
 
     def to_partner(self, half, name, spot):
-        self.chip_copies[half, name] = self.copies.start(self.send_buf.at[half, spot], self.chip_buf.at[half, spot], self.place.partner)
+        self.chip_copies[half, name] = self.copies.start(self.send_buf.at[half, spot], self.chip_buf.at[half, spot], self.place.partner,
+                                                              ('chip', self.m), self.send_buf)
 
     def p1(self):
         for half in (0, 1):
@@ -134,12 +147,13 @@
             add_rows(self.own_buf.at[half, spot, sub], self.own_buf.at[half, spot, sub], self.chip_buf.at[half, spot, sub])
 
     def ring(self, half, slot, spot, sub, by):
-        self.first[half, slot] = self.copies.start(self.own_buf.at[half, spot, sub], self.ring_buf.at[half, slot], self.place.on_ring(half, by))
+        self.first[half, slot] = self.copies.start(self.own_buf.at[half, spot, sub], self.ring_buf.at[half, slot], self.place.on_ring(half, by),
+                                                    ('ring', self.m), self.ring_buf)
 
     def tail(self, half, slot, spot, sub, by):
         here = self.spots[half][0]
         self.second[half, slot] = self.copies.start(self.own_buf.at[half, here, sub, spot], self.tail_buf.at[half, slot],
-                                                    self.place.on_ring(1 - half, by))
+                                                    self.place.on_ring(1 - half, by), ('tail', self.m), self.tail_buf)
 
     def p2(self):
         for half in (0, 1):
@@ -207,27 +221,30 @@
 
 
 class AllGather:
-    def __init__(self, place, copies, arrays):
-        self.place, self.copies = place, copies
+    def __init__(self, place, copies, arrays, tag):
+        self.place, self.copies, self.tag = place, copies, tag
+        self.arrays = arrays
         self.coords = (place.x, place.y)
-        self.jobs = [(array, half) for array in arrays for half in (0, 1)]
-        self.first, self.second, self.tails, self.last = {}, {}, {}, []
-
-    def send(self, job, spot, other, sub, axis, by):
-        array, half = job
+        self.jobs = [(array, half, i) for i, array in enumerate(arrays) for half in (0, 1)]
+        self.first, self.second = {}, {}
+
+    def send(self, job, spot, other, sub, axis, by, kind):
+        array, half, i = job
+        total = {'first': array.at[0, 0:3, 0], 'second': array.at[0], 'sub': array.at[0, 0:2]}[kind]
         yy, xx = (other, spot) if half == 0 else (spot, other)
         half_cols = array.shape[-1] // 2
         cols = pl.ds(half * half_cols, half_cols) if sub is None else pl.ds(half * half_cols + sub * half_cols // 2, half_cols // 2)
         ref = array.at[yy, xx, self.place.core, :, cols]
-        return self.copies.start(ref, ref, self.place.on_ring(axis, by))
+        return self.copies.start(ref, ref, self.place.on_ring(axis, by), (kind, self.tag, i), total,
+                                 (kind, self.tag, i) if kind == 'sub' else None)
 
     def send_line(self, job, other):
-        array, half = job
+        array, half, i = job
         half_cols = array.shape[-1] // 2
         cols = pl.ds(half * half_cols, half_cols)
         core = self.place.core
         ref = array.at[other, :, core, :, cols] if half == 0 else array.at[:, other, core, :, cols]
-        self.last.append(self.copies.start(ref, ref, self.place.partner))
+        self.copies.start(ref, ref, self.place.partner, ('line', self.tag, i), array.at[0:2], ('line', self.tag, i))
 
     def each(self):
         for j, job in enumerate(self.jobs):
@@ -237,9 +254,9 @@
     def a0(self):
         for j, job, half, spot, other in self.each():
             for by in (1, -1, 2):
-                self.first[j, by] = self.send(job, spot, other, None, half, by)
+                self.first[j, by] = self.send(job, spot, other, None, half, by, 'first')
             for by in (1, -1):
-                self.second[j, 0, by] = self.send(job, spot, other, None, 1 - half, by)
+                self.second[j, 0, by] = self.send(job, spot, other, None, 1 - half, by, 'second')
 
     def a1(self):
         for j, job, half, spot, other in self.each():
@@ -247,14 +264,14 @@
                 self.first[j, by].wait_recv()
                 came = self.place.shift(spot, -by)
                 for to in (1, -1):
-                    self.second[j, -by, to] = self.send(job, came, other, None, 1 - half, to)
+                    self.second[j, -by, to] = self.send(job, came, other, None, 1 - half, to, 'second')
 
     def a2(self):
         for j, job, half, spot, other in self.each():
             self.first[j, 2].wait_recv()
             far = self.place.shift(spot, 2)
             for to in (1, -1):
-                self.second[j, 2, to] = self.send(job, far, other, None, 1 - half, to)
+                self.second[j, 2, to] = self.send(job, far, other, None, 1 - half, to, 'second')
             self.send_line(job, other)
 
     def a3(self):
@@ -266,7 +283,7 @@
             for to, sub in ((1, 0), (-1, 1)):
                 self.second[j, off, to].wait_recv()
                 came = self.place.shift(other, -to)
-                self.tails[j, off, to] = self.send(job, self.place.shift(spot, off), came, sub, 1 - half, to)
+                self.send(job, self.place.shift(spot, off), came, sub, 1 - half, to, 'sub')
 
     def a4(self):
         self.pass_on(2)
@@ -275,27 +292,26 @@
                 self.send_line(job, self.place.shift(other, to))
 
     def a5(self):
+        for i, array in enumerate(self.arrays):
+            self.copies.wait_group(('sub', self.tag, i), array.at[0, 0:2])
         for j, job, half, spot, other in self.each():
-            for off in (0, 1, -1, 2):
-                for to in (1, -1):
-                    self.tails[j, off, to].wait_recv()
             self.send_line(job, self.place.shift(other, 2))
 
     def a6(self):
-        for copy in self.last:
-            copy.wait_recv()
+        for i, array in enumerate(self.arrays):
+            self.copies.wait_group(('line', self.tag, i), array.at[0:2])
 
 
 def all_reduce(place, copies, value, pair_buf, ring_bufs, out):
     side = place.side
-    copy = copies.start(value, pair_buf, place.partner)
+    copy = copies.start(value, pair_buf, place.partner, 'pair', value)
     copy.wait_recv()
     total = value[...] + pair_buf[...]
     for axis in (0, 1):
         coord = place.x if axis == 0 else place.y
         buf = ring_bufs.at[axis]
         buf[coord] = total
-        going = [copies.start(buf.at[coord], buf.at[coord], place.on_ring(axis, by)) for by in (1, -1, 2)]
+        going = [copies.start(buf.at[coord], buf.at[coord], place.on_ring(axis, by), ('all', axis), buf.at[0:3]) for by in (1, -1, 2)]
         for copy in going:
             copy.wait_recv()
         total = buf[0]
@@ -459,8 +475,9 @@
     scratch += [pltpu.VMEM(item.shape[1:], B16) for item in right + weights] + [pltpu.SemaphoreType.DMA((max(1, len(right) + n_weights),))]
     if total_reduce:
         scratch += [pltpu.VMEM((8, width), F32), pltpu.VMEM((8, width), F32), pltpu.VMEM((2, side, 8, width), F32)]
-    n_sems = micro * (48 * n_full + (32 if reduces else 0)) + (7 if total_reduce else 0)
-    scratch += post_scratch + [pltpu.SemaphoreType.DMA((n_sems,)), pltpu.SemaphoreType.DMA((n_sems,))]
+    n_send = micro * (4 * n_full + (3 if reduces else 0)) + (3 if total_reduce else 0)
+    n_recv = micro * (24 * n_full + (32 if reduces else 0)) + (7 if total_reduce else 0)
+    scratch += post_scratch + [pltpu.SemaphoreType.DMA((n_send,)), pltpu.SemaphoreType.DMA((n_recv,))]
     n_rows, n_extra, n_grads, n_right, n_kept = len(row_ins), len(extra), len(grads), len(right), len(kept)
     has_gain = gain is not None
 
@@ -540,8 +557,8 @@
                 weight_grad_rows(m, rows_v, post_refs[1][m], work[2], post_refs[3], 512)
                 weight_grad(m, work[0][...], rows_of(full_bufs[-1], m), work[3], post_refs[4], None, 512)
 
-        early = [AllGather(place, copies, [buf.at[m] for buf in full_bufs[:n_extra]]) for m in range(micro)]
-        late = [AllGather(place, copies, [full_bufs[-1].at[m]] if new_full else []) for m in range(micro)]
+        early = [AllGather(place, copies, [buf.at[m] for buf in full_bufs[:n_extra]], ('early', m)) for m in range(micro)]
+        late = [AllGather(place, copies, [full_bufs[-1].at[m]] if new_full else [], ('late', m)) for m in range(micro)]
         first_early = not new_full
 
         def early_step(name, when):

time: 550 us -> 530 us (0.964)
  Pallas kernels: 526 us -> 506 us
    pallas_call x9, Pallas kernels: 526 us -> 506 us  [stage_call(): pl.pallas_call(body, out_shape=outs, in_specs=in_specs, out_specs=[vmem]...]
where the time goes in v3:
time: 530 us; the launch traced here: 525 us
  Pallas kernels  506 us (95%)
  other arithmetic  9.18 us (2%)
  local copies, waits for them, and re-layouts  7.92 us (1%)
    pallas_call x9, Pallas kernels, stage_call(): pl.pallas_call(body, out_shape=outs, in_specs=in_specs, out_specs=[vmem]...  506 us

profile of v3, /device:TPU:97, one launch (start us, length us, event | category | flops | bytes accessed | tf_op | source)
XLA Modules:
  0.0 524.5 jit_solution(8996851203003228845)
XLA Ops:
  0.6 1.4 fusion.2
  2.0 1.4 fusion.1
  3.5 32.0 %stage_norm_0.1 = (bf16[2,16,2048]{2,1,0:T(8,128)(2,1)}, bf16[2,512,64]{2,1,0:T(8,128)(2,1)}, bf16[2,512,64]{2,1,0:T(8,128)(2,1)}, bf16[2,512,64]{2,1,0:T(8,128)...) custom-call(bf16[2,16,2048]{2,1,0:T(8,128)(2,1)} %refs_4_.7, f32[1,2048]{1,0:T(1,128)} %get-tuple-element.119.refs_1_.refs_6_, ...), custom_call_target="tpu_custom_call" | custom-call | tf_op jit(solution)/shard_map/stage_norm_0/pallas_call | solution.py:650
  35.4 51.9 %stage_fwd_1.1 = (bf16[2,16,2048]{2,1,0:T(8,128)(2,1)}, bf16[2,16,2048]{2,1,0:T(8,128)(2,1)}, bf16[2,512,256]{2,1,0:T(8,128)(2,1)}) custom-call(bf16[2,16,2,16,64]{4,3,2,1,0:T(8,128)(2,1)} %bitcast.48, bf16[2,64,2048]{2,1,0:T(8,128)(2,1)} %bitcast.44, bf16[2,16,2048]{2,1,0:T(8,128)(2,1)} %refs_4_.7, f32[1,2048]{1,0:T(1,128)} %get-tuple-element.117.refs_3_.refs_6_, ...), custom_call_target="tpu_custom_call" | custom-call | tf_op jit(solution)/shard_map/stage_fwd_1/pallas_call | solution.py:650
  87.3 54.5 %stage_fwd_2.1 = (bf16[2,16,2048]{2,1,0:T(8,128)(2,1)}, bf16[2,16,2048]{2,1,0:T(8,128)(2,1)}, bf16[2,512,64]{2,1,0:T(8,128)(2,1)}, bf16[2,512,64]{2,1,0:T(8,128)...) custom-call(bf16[2,16,2,16,256]{4,3,2,1,0:T(8,128)(2,1)} %bitcast.62, ...), custom_call_target="tpu_custom_call" | custom-call | tf_op jit(solution)/shard_map/stage_fwd_2/pallas_call | solution.py:650
  141.8 52.2 %stage_fwd_3.1 = (bf16[2,16,2048]{2,1,0:T(8,128)(2,1)}, bf16[2,16,2048]{2,1,0:T(8,128)(2,1)}, bf16[2,512,256]{2,1,0:T(8,128)(2,1)}) custom-call(bf16[2,16,2,16,64]{4,3,2,1,0:T(8,128)(2,1)} %bitcast.49, bf16[2,64,2048]{2,1,0:T(8,128)(2,1)} %bitcast.45, bf16[2,16,2048]{2,1,0:T(8,128)(2,1)} %get-tuple-element.61.refs_2_.refs_4_, ...), custom_call_target="tpu_custom_call" | custom-call | tf_op jit(solution)/shard_map/stage_fwd_3/pallas_call | solution.py:650
  194.0 63.9 %stage_fwd_last_4.1 = (bf16[2,16,2048]{2,1,0:T(8,128)(2,1)}, bf16[2,512,256]{2,1,0:T(8,128)(2,1)}, bf16[2,512,256]{2,1,0:T(8,128)(2,1)}, bf16[2048,256]{1,0:T(8,...) custom-call(bf16[2,16,2,16,256]{4,3,2,1,0:T(8,128)(2,1)} %bitcast.63, bf16[2,256,2048]{2,1,0:T(8,128)(2,1)} %refs_10_.1, ...), custom_call_target="tpu_custom_call" | custom-call | tf_op jit(solution)/shard_map/stage_fwd_last_4/pallas_call | solution.py:650
  257.9 68.9 %stage_bwd_5.1 = (bf16[2,16,2048]{2,1,0:T(8,128)(2,1)}, f32[1,2048]{1,0:T(1,128)}, bf16[2,512,64]{2,1,0:T(8,128)(2,1)}, bf16[2,512,64]{2,1,0:T(8,128)(2,1)}, bf1...) custom-call(bf16[2,16,2,16,256]{4,3,2,1,0:T(8,128)(2,1)} %bitcast.60, ...), custom_call_target="tpu_custom_call" | custom-call | tf_op jit(solution)/shard_map/stage_bwd_5/pallas_call | solution.py:650
  326.8 67.4 %stage_bwd_6.1 = (bf16[2,16,2048]{2,1,0:T(8,128)(2,1)}, f32[1,2048]{1,0:T(1,128)}, bf16[2,512,256]{2,1,0:T(8,128)(2,1)}, bf16[2,512,256]{2,1,0:T(8,128)(2,1)}, b...) custom-call(bf16[2,16,2,16,64]{4,3,2,1,0:T(8,128)(2,1)} %bitcast.64, ...), custom_call_target="tpu_custom_call" | custom-call | tf_op jit(solution)/shard_map/stage_bwd_6/pallas_call | solution.py:650
  394.2 69.4 %stage_bwd_7.1 = (bf16[2,16,2048]{2,1,0:T(8,128)(2,1)}, f32[1,2048]{1,0:T(1,128)}, bf16[2,512,64]{2,1,0:T(8,128)(2,1)}, bf16[2,512,64]{2,1,0:T(8,128)(2,1)}, bf1...) custom-call(bf16[2,16,2,16,256]{4,3,2,1,0:T(8,128)(2,1)} %bitcast.58, ...), custom_call_target="tpu_custom_call" | custom-call | tf_op jit(solution)/shard_map/stage_bwd_7/pallas_call | solution.py:650
  463.6 46.4 %stage_bwd_last_8.1 = (bf16[2,16,2048]{2,1,0:T(8,128)(2,1)}, f32[8,2048]{1,0:T(8,128)}) custom-call(bf16[2,16,2,16,64]{4,3,2,1,0:T(8,128)(2,1)} %bitcast.69, bf16[2,16,2,16,64]{4,3,2,1,0:T(8,128)(2,1)} %bitcast.70, bf16[2,16,2,16,64]{4,3,2,1,0:T(8,128)(2,1)} %bitcast.71, bf16[2,3,64,2048]{3,2,1,0:T(8,128)(2,1)} %bitcast.43, bf16[2,16,2048]{2,1,0:T(8,128)(2,1)} %refs_4_.7, ...), custom_call_target="tpu_custom_call" | custom-call | tf_op jit(solution)/shard_map/stage_bwd_last_8/pallas_call | solution.py:650
  510.0 1.5 slice.31
  511.4 0.9 fusion
  512.4 0.6 pad_maximum_fusion.3
  513.0 0.0 copy-start
  513.0 2.0 maximum_bitcast_fusion.1
  515.0 2.7 maximum_bitcast_fusion
  517.7 0.0 copy-done
  517.7 0.0 copy-done.1
  517.7 0.0 copy-start.3
  517.7 0.0 copy-start.4
  517.7 0.0 copy-start.5
  517.7 1.5 pad_maximum_fusion.2
  519.2 0.0 copy-done.2
  519.2 0.8 copy-done.3
  520.0 0.3 copy-done.4
  520.3 0.3 copy-done.5
  520.6 2.4 pad_maximum_fusion
  523.0 0.0 copy-done.6
  523.0 0.7 copy.23
  523.7 0.0 copy-done.7
  523.7 0.7 copy.24
  (4 shorter events, 0.0 us)
Async XLA Ops:
  513.0 4.7 copy-start
  513.0 4.7 copy-start.1
  517.7 1.5 copy-start.2
  517.7 2.3 copy-start.3
  517.7 2.6 copy-start.4
  517.7 2.9 copy-start.5
  520.6 2.4 copy-start.6
  520.6 3.0 copy-start.7
